TPU v7x, 32 devices: a whole 2x2x4 slice. The times are simulated.
32 devices in a mesh: gx: 4 (over z), gy: 8 (over y, x, core).
Axes of the slice: x: 2, y: 2, z: 4, core: 2. Of those that a mesh axis runs over, the one named last changes fastest.
Arguments:
- tokens: bfloat16 [28672, 4096], P(('gx', 'gy')), may hold values from -6 to 6
- codes: bfloat16 [4096, 512], P(('gx', 'gy')), may hold values from -0.09375 to 0.09375
- scales: float32 [128, 4], P(('gx', 'gy')), may hold values from 0.5 to 2
- gain: float32 [128], replicated, may hold values from 0.1 to 1.9
- cotangent: bfloat16 [28672, 512], P(('gx', 'gy')), may hold values from -96 to 96
Outputs:
- keys: bfloat16 [28672, 512], P(('gx', 'gy'))
- token_grad: bfloat16 [28672, 4096], P(('gx', 'gy'))
- weight_grad: float32 [4096, 512], P(('gx', 'gy'))
All inputs are finite; a program needn't handle non-finite values.
Results may differ from a plain program's by a relative error of at most 0.019.
Values may be sent and summed in bfloat16 or wider, within the bound.
No kernel may reach another device: no remote copies, remote signals or barrier semaphores. Data moves between devices by JAX's collectives and lax.ppermute only.
A program may use at most 128 MiB of HBM per device.

v0:
```python
import math

import jax
import jax.numpy as jnp
from jax import lax
from jax.sharding import PartitionSpec as P

KV_HEADS = 4
HEAD = 128
QBLK = 32


clip_ratio = 2.5


def hadamard(length):
    indices = jnp.arange(length, dtype=jnp.int32)
    common = jnp.bitwise_and(indices[:, None], indices[None, :])
    parity = jnp.zeros((length, length), jnp.int32)
    for position in range(length.bit_length() - 1):
        parity = parity + jnp.bitwise_and(jnp.right_shift(common, position), 1)
    return (1 - 2 * (parity % 2)).astype(jnp.float32) / math.sqrt(length)


def rotate(matrix, rotation):
    shaped = matrix.reshape(matrix.shape[0], KV_HEADS, HEAD)
    rotated = jnp.einsum("rhc,cd->rhd", shaped, rotation, precision=lax.Precision.HIGHEST)
    return rotated.reshape(matrix.shape)


def clipped(matrix):
    shaped = matrix.reshape(matrix.shape[0] // QBLK, QBLK, KV_HEADS, HEAD)
    mean_square = jnp.mean(shaped * shaped, axis=(1, 3), keepdims=True)
    clip_bound = clip_ratio * jnp.sqrt(mean_square + 1e-06)
    return jnp.clip(shaped, -clip_bound, clip_bound).reshape(matrix.shape)


def normed_keys(projected, gain):
    shaped = projected.reshape(projected.shape[0], KV_HEADS, HEAD)
    mean_square = jnp.mean(shaped * shaped, axis=-1, keepdims=True)
    return (shaped * lax.rsqrt(mean_square + 1e-06) * gain).reshape(projected.shape)


def scaled(values, block_scales):
    block_count = block_scales.shape[0]
    blocks = values.astype(jnp.float32).reshape(
        block_count, values.shape[0] // block_count, KV_HEADS, HEAD
    )
    return (blocks * block_scales[:, None, :, None]).reshape(values.shape).astype(jnp.bfloat16)


def collect(pieces):
    outer_count = lax.axis_size("gx")
    inner_count = lax.axis_size("gy")
    near_rows = lax.all_gather(pieces, "gx", axis=0, tiled=True)
    gathered = lax.all_gather(near_rows, "gy", axis=0, tiled=True)
    shaped = gathered.reshape(
        (inner_count, outer_count, gathered.shape[0] // (inner_count * outer_count))
        + gathered.shape[1:]
    )
    return jnp.swapaxes(shaped, 0, 1).reshape(gathered.shape)


def body(tokens, codes, scales, gain, cotangent):
    weight = collect(scaled(codes, scales))
    projected = jnp.dot(tokens, weight, preferred_element_type=jnp.float32)
    normed, pullback = jax.vjp(lambda value_in: normed_keys(value_in, gain), projected)
    keys_out = normed.astype(jnp.bfloat16)
    key_grad = pullback(cotangent.astype(jnp.float32))[0].astype(jnp.bfloat16)
    token_grad = lax.dot_general(
        key_grad, weight, (((1,), (1,)), ((), ())), preferred_element_type=jnp.float32
    ).astype(jnp.bfloat16)
    rotation = hadamard(HEAD)
    partial_value = lax.dot_general(
        tokens, key_grad, (((0,), (0,)), ((), ())), preferred_element_type=jnp.float32
    )
    level_one = lax.psum_scatter(
        clipped(rotate(partial_value, rotation)).astype(jnp.bfloat16),
        "gx",
        scatter_dimension=0,
        tiled=True,
    ).astype(jnp.float32)
    recoded = clipped(level_one)
    level_two = lax.psum_scatter(
        recoded.astype(jnp.bfloat16), "gy", scatter_dimension=0, tiled=True
    ).astype(jnp.float32)
    weight_grad = rotate(level_two, rotation)
    return (keys_out, token_grad, weight_grad)


def solution(mesh):
    in_specs = (
        P(("gx", "gy"), None),
        P(("gx", "gy"), None),
        P(("gx", "gy"), None),
        P(),
        P(("gx", "gy"), None),
    )
    out_specs = (P(("gx", "gy"), None), P(("gx", "gy"), None), P(("gx", "gy"), None))
    return jax.shard_map(body, mesh=mesh, in_specs=in_specs, out_specs=out_specs, check_vma=False)
```

profile of v0, /device:TPU:0, one launch (start us, length us, event | category | flops | bytes accessed | tf_op | source)
XLA Modules:
  0.0 265.3 jit_solution(8661850951664697459)
XLA Ops:
  7.2 0.0 all-gather.2.cloned.1.call-start
  7.2 0.8 mul.121
  8.0 0.9 fusion.7
  8.9 18.0 %all_gather.6 = bf16[512,512]{1,0:T(8,128)(2,1)} all-gather(bf16[128,512]{1,0:T(8,128)(2,1)S(1)} %fusion.7), channel_id=1, replica_groups=mesh['gx'=4,'gy'=8] {'gx'}, dimensions={0}, use_global_device_ids=true | all-gather | bytes 655360 | tf_op jit(solution)/shard_map/all_gather | solution.py:55
  26.9 0.0 all-gather.2.cloned.1.call-update
  27.0 0.0 reduce-scatter.3.cloned.1.call-start
  27.0 1.5 copy.21
  28.6 0.7 broadcast_bitcast_fusion
  29.2 36.4 %all-gather.2.cloned.1.call-done = bf16[4096,512]{1,0:T(8,128)(2,1)} async-done(((bf16[512,512]{1,0:T(8,128)(2,1)}), bf16[4096,512]{1,0:T(8,128)(2,1)}) %all-gather.2.cloned.1.call-update) | async-done | bytes 4194320 | tf_op jit(solution)/shard_map/all_gather | solution.py:56
  65.6 0.0 copy-start.1
  65.6 0.0 copy-start.6
  65.6 2.7 %copy.20 = bf16[4,8,128,512]{3,2,1,0:T(8,128)(2,1)S(1)} copy(bf16[4,8,128,512]{3,2,0,1:T(8,128)(2,1)} %bitcast.72) | data formatting | bytes 8388608 | tf_op jit(solution)/shard_map/transpose | solution.py:61
  68.3 0.0 copy-start
  68.3 3.2 %copy-done.1 = bf16[896,4096]{1,0:T(8,128)(2,1)S(1)} copy-done((bf16[896,4096]{1,0:T(8,128)(2,1)S(1)}, bf16[896,4096]{1,0:T(8,128)(2,1)}, u32[]{:S(2)}) %copy-start.1) | copy-done | bytes 7340056
  71.4 0.0 copy-done.6
  71.4 4.7 %multiply_reduce_fusion.1 = (f32[896,4]{0,1:T(4,128)S(1)}, f32[896,4]{0,1:T(4,128)S(1)}, f32[512,896]{1,0:T(8,128)S(1)}) fusion(f32[128]{0:T(128)S(1)} %copy-done.6, bf16[896,512]{0,1:T(8,128)(2,1)S(1)} %copy.21, bf16[4096,512]{1,0:T(8,128)(2,1)S(1)} %bitcast.70, bf16[896,4096]{1,0:T(8,128)(2,1)S(1)} %copy-done.1), kind=kOutput, calls=%fused_computation.18 | convolution fusion | flops 3760841728 | bytes 14316032 | tf_op jit(solution)/shard_map/dot_general | solution.py:66
  76.2 0.0 copy-done
  76.2 1.5 fusion.4
  77.7 0.0 copy-start.4
  77.7 0.9 copy-done.4
  78.7 6.7 %convolution_bitcast_fusion = f32[4096,512]{0,1:T(8,128)} fusion(bf16[896,512]{0,1:T(8,128)(2,1)S(1)} %get-tuple-element.14, bf16[896,4096]{1,0:T(8,128)(2,1)S(1)} %copy-done.1), kind=kOutput, calls=%fused_computation.5 | convolution fusion | flops 3758096384 | bytes 16646144 | tf_op jit(solution)/shard_map/dot_general | solution.py:74
  85.3 9.0 %copy.22 = f32[4096,512]{1,0:T(8,128)} copy(f32[4096,512]{0,1:T(8,128)} %convolution_bitcast_fusion) | data formatting | bytes 16777216 | tf_op jit(solution)/shard_map/dot_general | solution.py:74
  94.3 9.9 %dot_general.26 = f32[128,32,4,128]{3,2,1,0:T(4,128)} reshape(f32[4096,512]{1,0:T(8,128)} %copy.22) | data formatting | bytes 16777216 | tf_op jit(solution)/shard_map/rhc,cd->rhd/dot_general | solution.py:27
  104.2 16.1 %multiply_reduce_fusion = (f32[128,4]{0,1:T(4,128)S(1)}, bf16[128,32,4,128]{0,3,2,1:T(8,128)(2,1)S(1)}) fusion(f32[128,32,4,128]{3,2,1,0:T(4,128)} %dot_general.26), kind=kOutput, calls=%fused_computation.3 | convolution fusion | flops 3228106240 | bytes 12584960 | tf_op jit(solution)/shard_map/rhc,cd->rhd/dot_general | solution.py:27
  120.4 2.3 minimum_convert_fusion
  122.7 7.9 %copy.24 = bf16[128,32,4,128]{3,2,1,0:T(4,128)(2,1)} copy(bf16[128,32,4,128]{0,3,2,1:T(8,128)(2,1)} %minimum_convert_fusion) | data formatting | bytes 8388608 | tf_op jit(solution)/shard_map/convert_element_type | solution.py:78
  130.7 4.9 %copy.43 = bf16[512,8,4,128]{3,1,2,0:T(8,128)(2,1)} copy(bf16[512,8,4,128]{3,2,1,0:T(4,128)(2,1)} %bitcast.69) | data formatting | bytes 8388608
  135.6 0.0 reduce-scatter.3.cloned.1.call-update
  135.6 0.0 reduce-scatter.5.cloned.1.call-start
  135.7 76.9 %reduce-scatter.3.cloned.1.call-done = bf16[1024,512]{1,0:T(8,128)(2,1)} async-done(((bf16[4096,512]{1,0:T(8,128)(2,1)}), bf16[1024,512]{1,0:T(8,128)(2,1)}) %reduce-scatter.3.cloned.1.call-update) | async-done | bytes 1048592 | tf_op jit(solution)/shard_map/reduce_scatter | solution.py:77
  212.6 2.8 %convert_multiply_fusion = f32[1024,512]{1,0:T(8,128)} fusion(bf16[1024,512]{1,0:T(8,128)(2,1)} %reduce-scatter.3.cloned.1.call-done), kind=kLoop, calls=%fused_computation.11 | loop fusion | flops 1048576 | bytes 3145728 | tf_op jit(solution)/shard_map/mul | solution.py:33
  215.4 0.0 copy-start.2
  215.4 2.0 mul.146
  217.4 0.4 reduce_sum.43
  217.8 0.0 copy-start.3
  217.8 0.3 min.29
  218.2 0.0 copy-start.5
  218.2 0.3 max.29
  218.5 0.0 copy-done.2
  218.5 1.4 fusion.3
  220.0 0.0 reduce-scatter.5.cloned.1.call-update
  220.0 0.0 copy-done.3
  220.0 1.3 copy.27
  221.3 0.0 copy-done.5
  221.3 9.3 %convolution_convert_fusion = bf16[896,4096]{1,0:T(8,128)(2,1)} fusion(bf16[896,512]{0,1:T(8,128)(2,1)S(1)} %copy-done.5, bf16[4096,512]{1,0:T(8,128)(2,1)} %bitcast.71), kind=kOutput, calls=%fused_computation.4 | convolution fusion | flops 3761766400 | bytes 12451840 | tf_op jit(solution)/shard_map/dot_general | solution.py:70
  230.6 26.0 %reduce-scatter.5.cloned.1.call-done = bf16[128,512]{1,0:T(8,128)(2,1)} async-done(((bf16[1024,512]{1,0:T(8,128)(2,1)}), bf16[128,512]{1,0:T(8,128)(2,1)}) %reduce-scatter.5.cloned.1.call-update) | async-done | bytes 131088 | tf_op jit(solution)/shard_map/reduce_scatter | solution.py:84
  256.6 1.0 copy.25
  257.6 0.3 fusion.14
  258.0 0.8 copy.28
  (3 shorter events, 0.0 us)
Async XLA Ops:
  7.2 58.4 %all-gather.2.cloned.1.call-start = ((), (), s32[]{:S(2)}) async-start(), calls=%async_computation.2 | async-start | bytes 4718592 | tf_op jit(solution)/shard_map/all_gather | solution.py:56
  27.0 185.6 %reduce-scatter.3.cloned.1.call-start = ((), (), s32[]{:S(2)}) async-start(), calls=%async_computation.3 | async-start | bytes 5242880 | tf_op jit(solution)/shard_map/reduce_scatter | solution.py:77
  65.6 5.9 %copy-start.1 = (bf16[896,4096]{1,0:T(8,128)(2,1)S(1)}, bf16[896,4096]{1,0:T(8,128)(2,1)}, u32[]{:S(2)}) copy-start(bf16[896,4096]{1,0:T(8,128)(2,1)} %param.5) | copy-start | bytes 22020100
  65.6 5.9 %copy-start.6 = (f32[128]{0:T(128)S(1)}, f32[128]{0:T(128)}, u32[]{:S(2)}) copy-start(f32[128]{0:T(128)} %param.8) | copy-start | bytes 1540
  68.3 7.9 %copy-start = (bf16[4,8,128,512]{3,2,1,0:T(8,128)(2,1)}, bf16[4,8,128,512]{3,2,1,0:T(8,128)(2,1)S(1)}, u32[]{:S(2)}) copy-start(bf16[4,8,128,512]{3,2,1,0:T(8,128)(2,1)S(1)} %copy.20) | copy-start | bytes 12582916
  77.7 0.9 copy-start.4
  135.6 121.0 %reduce-scatter.5.cloned.1.call-start = ((), (), s32[]{:S(2)}) async-start(), calls=%async_computation.4 | async-start | bytes 1179648 | tf_op jit(solution)/shard_map/reduce_scatter | solution.py:84
  215.4 3.1 %copy-start.2 = (bf16[1024,512]{1,0:T(8,128)(2,1)S(1)}, bf16[1024,512]{1,0:T(8,128)(2,1)}, u32[]{:S(2)}) copy-start(bf16[1024,512]{1,0:T(8,128)(2,1)} %reduce-scatter.3.cloned.1.call-done) | copy-start | bytes 3145732
  217.8 2.2 copy-start.3
  218.2 3.1 %copy-start.5 = (bf16[896,512]{0,1:T(8,128)(2,1)S(1)}, bf16[896,512]{0,1:T(8,128)(2,1)}, u32[]{:S(2)}) copy-start(bf16[896,512]{0,1:T(8,128)(2,1)} %copy-done.4) | copy-start | bytes 2752516
Sparse Core Ops, SparseCore 0:
  27.1 38.4 all-gather.1
  135.7 76.7 reduce-scatter.2
  220.1 36.4 reduce-scatter.4
where the time goes:
time: 266 us; the launch traced here: 265 us
  waiting for transfers between devices  139 us (52%)
  local copies, waits for them, and re-layouts  47.4 us (18%)
  matrix products  37.1 us (14%)
  blocking collectives  18 us (7%)
  between operations  13.9 us (5%)
  other arithmetic  9.49 us (4%)
    reduce_scatter x1, waiting for transfers between devices, body(): lax.psum_scatter(clipped(rotate(partial_value, rotation)).astype(jnp.bflo...  76.9 us
    all_gather x1, waiting for transfers between devices, collect(): gathered = lax.all_gather(near_rows, 'gy', axis=0, tiled=True)  36.4 us
    reduce_scatter x1, waiting for transfers between devices, body(): lax.psum_scatter(recoded.astype(jnp.bfloat16), 'gy', scatter_dimension=0,...  26 us
    all_gather x1, blocking collectives, collect(): near_rows = lax.all_gather(pieces, 'gx', axis=0, tiled=True)  18 us
    dot_general x2, matrix products, rotate(): jnp.einsum('rhc,cd->rhd', shaped, rotation, precision=lax.Precision.HIGHEST)  16.4 us
    unnamed x18, local copies, waits for them, and re-layouts  12.7 us
    dot_general x1, local copies, waits for them, and re-layouts, rotate(): jnp.einsum('rhc,cd->rhd', shaped, rotation, precision=lax.Precision.HIGHEST)  9.9 us
    dot_general x1, matrix products, body(): lax.dot_general(key_grad, weight, (((1,), (1,)), ((), ())), preferred_ele...  9.27 us
  transfers between devices with their start and end apart: 3, of which 3 were waited for; matrix products, arithmetic and copies ran while one was open for 5% of the time, Pallas kernels for 0%

commit v1 on v0

v1 whole, which is shorter than its diff:
```python
import math

import jax
import jax.numpy as jnp
import numpy as np
from jax import lax
from jax.experimental import pallas as pl
from jax.experimental.pallas import tpu as pltpu
from jax.sharding import PartitionSpec as P


HEAD = 128
QBLK = 32
TG_PARTS = 4
CLIP = 2.5
EPS = 1e-06


f32 = jnp.float32
bf16 = jnp.bfloat16
HI = lax.Precision.HIGHEST
BIG = pltpu.CompilerParams(vmem_limit_bytes=60 * 1024 * 1024)


def signs(length):
    idx = np.arange(length)
    common = idx[:, None] & idx[None, :]
    parity = np.zeros((length, length), np.int64)
    for pos in range(length.bit_length() - 1):
        parity += (common >> pos) & 1
    return (1 - 2 * (parity % 2)).astype(np.float32)


def block_mean_matrix(rows):
    lane = np.arange(128)
    return ((lane[:, None] // QBLK) == (lane[None, :] // QBLK)).astype(np.float32) / (QBLK * rows)


def three_parts(x):
    high = x.astype(bf16)
    rest = x - high.astype(f32)
    middle = rest.astype(bf16)
    low = (rest - middle.astype(f32)).astype(bf16)
    return jnp.concatenate([high, middle, low], axis=0)


def clipped_tiles(value, mean_matrix):
    heads = value.shape[0] // HEAD
    groups = value.shape[1] // 128
    tiles = [
        value[h * HEAD : (h + 1) * HEAD, g * 128 : (g + 1) * 128] for h in range(heads) for g in range(groups)
    ]
    rows = [jnp.sum(x * x, axis=0, keepdims=True) for x in tiles]
    pad = -len(rows) % 8
    if pad:
        rows.append(jnp.zeros((pad, 128), f32))
    squares = jnp.concatenate(rows, axis=0)
    count = squares.shape[0]
    parts = jnp.dot(three_parts(squares), mean_matrix, preferred_element_type=f32)
    means = parts[:count] + parts[count : 2 * count] + parts[2 * count :]
    bounds = CLIP * jnp.sqrt(means + EPS)
    for at, x in enumerate(tiles):
        limit = bounds[at : at + 1]
        yield at // groups, at % groups, jnp.minimum(jnp.maximum(x, -limit), limit).astype(bf16)


def scale_kernel(scales_ref, codes_ref, out_ref):
    blocks = codes_ref.shape[0] // QBLK
    heads = codes_ref.shape[1] // HEAD
    for b in range(blocks):
        for h in range(heads):
            tile = codes_ref[b * QBLK : (b + 1) * QBLK, h * HEAD : (h + 1) * HEAD].astype(f32)
            out_ref[b * QBLK : (b + 1) * QBLK, h * HEAD : (h + 1) * HEAD] = (tile * scales_ref[b, h]).astype(bf16)


def scaled(codes, scales):
    return pl.pallas_call(
        scale_kernel,
        out_shape=jax.ShapeDtypeStruct(codes.shape, bf16),
        in_specs=[pl.BlockSpec(memory_space=pltpu.SMEM), pl.BlockSpec(memory_space=pltpu.VMEM)],
        out_specs=pl.BlockSpec(memory_space=pltpu.VMEM),
        name="scale_rows",
    )(scales, codes)


def main_kernel(n, m, r, ra, where_ref, tok_hbm, gain_ref, cot_ref, had_ref, mean_ref, *refs):
    count = m + 2 * n
    pieces = refs[:count]
    keys_ref, kg_ref, qt_ref, term_ref, w_hbm, tv, wv, acc, tsem, wsem, osem = refs[count:]
    gi, gj, side = where_ref[0], where_ref[1], where_ref[2]
    d_model = tv.shape[1]
    heads = acc.shape[1] // HEAD
    kc = 1024
    steps = d_model // kc
    token_copies = [
        pltpu.make_async_copy(tok_hbm.at[:, pl.ds(c * kc, kc)], tv.at[:, pl.ds(c * kc, kc)], tsem.at[c])
        for c in range(steps)
    ]
    weight_copies = []

    def slab(piece, at, a, s, start, length):
        row = lax.rem(gi - a + n, n) * m + jnp.bitwise_xor(gj, s)
        off = pl.multiple_of(row * r + start, 16)
        weight_copies.append(
            pltpu.make_async_copy(piece.at[at], wv.at[pl.ds(off, length)], wsem.at[len(weight_copies)])
        )

    for s in range(m):
        for a in range(n):
            slab(pieces[s], a, a, s, 0, ra)
    for p in range(2 * n):
        for x in range(m // 2):
            slab(pieces[m + p], x, p // 2, 2 * x + p % 2, ra, r - ra)
    for c in weight_copies:
        c.start()
    for c in token_copies:
        c.start()
    for c in weight_copies:
        c.wait()
    w_out = pltpu.make_async_copy(wv, w_hbm, osem)
    w_out.start()
    for c in range(steps):
        token_copies[c].wait()
        part = jnp.dot(tv[:, c * kc : (c + 1) * kc], wv[c * kc : (c + 1) * kc], preferred_element_type=f32)
        if c == 0:
            acc[...] = part
        else:
            acc[...] += part
    gain = gain_ref[...]
    for h in range(heads):
        lanes = slice(h * HEAD, (h + 1) * HEAD)
        raw = acc[:, lanes]
        inv = lax.rsqrt(jnp.mean(raw * raw, axis=-1, keepdims=True) + EPS)
        unit = raw * inv
        keys_ref[:, lanes] = (unit * gain).astype(bf16)
        g = cot_ref[:, lanes].astype(f32) * gain
        kg = (inv * (g - unit * jnp.mean(g * unit, axis=-1, keepdims=True))).astype(bf16)
        kg_ref[:, lanes] = kg
        turned = lax.dot_general(had_ref[...], kg, (((1,), (1,)), ((), ())), preferred_element_type=f32)
        qt_ref[lanes, :] = (turned * (1.0 / math.sqrt(HEAD))).astype(bf16)
    width = term_ref.shape[2]
    bw = min(width, 512)
    for d in range(term_ref.shape[0]):
        row = jnp.where(side == 0, d, n - 1 - d)
        for b in range(width // bw):
            off = pl.multiple_of(row * width + b * bw, bw)
            value = jnp.dot(qt_ref[:HEAD], tv[:, pl.ds(off, bw)], preferred_element_type=f32)
            for _, g, x in clipped_tiles(value, mean_ref[...]):
                term_ref[d, :, b * bw + g * 128 : b * bw + (g + 1) * 128] = x
    w_out.wait()


def main_call(n, m, r, ra, where, tokens, gain, cot, had, mean, pieces):
    tok, d_model = tokens.shape
    kv = cot.shape[1]
    nd = n // 2
    vm = pl.BlockSpec(memory_space=pltpu.VMEM)
    hbm = pl.BlockSpec(memory_space=pltpu.HBM)
    return pl.pallas_call(
        lambda *a: main_kernel(n, m, r, ra, *a),
        out_shape=(
            jax.ShapeDtypeStruct((tok, kv), bf16),
            jax.ShapeDtypeStruct((tok, kv), bf16),
            jax.ShapeDtypeStruct((kv, tok), bf16),
            jax.ShapeDtypeStruct((nd, HEAD, m * r), bf16),
            jax.ShapeDtypeStruct((d_model, kv), bf16),
        ),
        in_specs=[pl.BlockSpec(memory_space=pltpu.SMEM), hbm, vm, vm, vm, vm] + [hbm] * len(pieces),
        out_specs=(vm, vm, vm, vm, hbm),
        scratch_shapes=[
            pltpu.VMEM((tok, d_model), bf16),
            pltpu.VMEM((d_model, kv), bf16),
            pltpu.VMEM((tok, kv), f32),
            pltpu.SemaphoreType.DMA((d_model // 1024,)),
            pltpu.SemaphoreType.DMA((2 * n * m,)),
            pltpu.SemaphoreType.DMA,
        ],
        compiler_params=BIG,
        name="project",
    )(where, tokens, gain, cot, had, mean, *pieces)


def term_kernel(skip, where_ref, tok_ref, qt_ref, mean_ref, *out_refs):
    rows = slice(skip * HEAD, (skip + len(out_refs)) * HEAD)
    value = jnp.dot(qt_ref[rows], tok_ref[...], preferred_element_type=f32)
    for h, g, x in clipped_tiles(value, mean_ref[...]):
        out_refs[h][0, :, g * 128 : (g + 1) * 128] = x


def term_call(n, m, r, where, tokens, qt, mean, first, skip, heads):
    tok = tokens.shape[0]
    kv = qt.shape[0]
    nd = n // 2
    width = m * r
    bw = min(1024, width)
    nb = width // bw

    def tok_index(d, b, where_ref):
        near = where_ref[2] == 0
        row = jnp.where(near if first else jnp.logical_not(near), d, n - 1 - d)
        return (0, row * nb + b)

    return pl.pallas_call(
        lambda *a: term_kernel(skip, *a),
        grid_spec=pltpu.PrefetchScalarGridSpec(
            num_scalar_prefetch=1,
            grid=(nd, nb),
            in_specs=[
                pl.BlockSpec((tok, bw), tok_index),
                pl.BlockSpec((kv, tok), lambda d, b, w: (0, 0)),
                pl.BlockSpec((128, 128), lambda d, b, w: (0, 0)),
            ],
            out_specs=[pl.BlockSpec((1, HEAD, bw), lambda d, b, w: (d, 0, b))] * heads,
        ),
        out_shape=[jax.ShapeDtypeStruct((nd, HEAD, width), bf16)] * heads,
        compiler_params=BIG,
        name="terms",
    )(where, tokens, qt, mean)


def tgrad_kernel(kg_ref, w_ref, *refs):
    refs[-1][...] = lax.dot_general(
        kg_ref[...], w_ref[...], (((1,), (1,)), ((), ())), preferred_element_type=f32
    ).astype(bf16)


def tgrad_call(kg, weight, filled, part, parts):
    tok, kv = kg.shape
    d_model = weight.shape[0]
    bw = 512
    steps = d_model // bw // parts
    base = part * steps
    extra = [] if filled is None else [filled]
    return pl.pallas_call(
        tgrad_kernel,
        grid=(steps,),
        in_specs=[
            pl.BlockSpec((tok, kv), lambda b: (0, 0)),
            pl.BlockSpec((bw, kv), lambda b: (base + b, 0)),
        ] + [pl.BlockSpec(memory_space=pltpu.HBM)] * len(extra),
        out_specs=pl.BlockSpec((tok, bw), lambda b: (0, base + b)),
        out_shape=jax.ShapeDtypeStruct((tok, d_model), bf16),
        input_output_aliases={2: 0} if extra else {},
        compiler_params=BIG,
        name="token_grad",
    )(kg, weight, *extra)


def recode_kernel(aligned, n, where_ref, a_ref, b_ref, mean_ref, keep_ref, send_ref):
    pair, parity = where_ref[1] // 2, lax.rem(where_ref[1], 2)

    @pl.when(jnp.logical_or(where_ref[0] == 0, where_ref[0] == n - 1))
    def _():
        for d in range(a_ref.shape[0]):
            value = a_ref[d].astype(f32) + b_ref[d].astype(f32)
            tiles = [x for _, _, x in clipped_tiles(value, mean_ref[...])]
            for g, x in enumerate(tiles):
                if not aligned:
                    keep_ref[d, :, g * 128 : (g + 1) * 128] = x
                elif g % 2 == 0:
                    at = jnp.bitwise_xor(pair, g // 2)
                    keep_ref[at, d] = jnp.where(parity == 0, x, tiles[g + 1])
                    send_ref[at, d] = jnp.where(parity == 0, tiles[g + 1], x)


def recode_call(n, m, r, where, arrived, mine, mean):
    aligned = r == 128
    vm = pl.BlockSpec(memory_space=pltpu.VMEM)
    nd = arrived.shape[0]
    shape = (m // 2, nd, HEAD, r) if aligned else arrived.shape
    keep, send = pl.pallas_call(
        lambda *a: recode_kernel(aligned, n, *a),
        out_shape=(jax.ShapeDtypeStruct(shape, bf16),) * 2,
        in_specs=[pl.BlockSpec(memory_space=pltpu.SMEM), vm, vm, vm],
        out_specs=(vm, vm),
        name="recode",
    )(where, arrived, mine, mean)
    if not aligned:
        pairs = jnp.bitwise_xor(where[1] // 2, jnp.arange(m // 2, dtype=jnp.int32))
        blocks = keep.reshape(nd, HEAD, m, r).transpose(2, 0, 1, 3)
        parity = where[1] % 2
        keep = jnp.take(blocks, pairs * 2 + parity, axis=0)
        send = jnp.take(blocks, pairs * 2 + 1 - parity, axis=0)
    return keep, send


def body(tokens, codes, scales, gain, cotangent):
    n = lax.axis_size("gx")
    m = lax.axis_size("gy")
    gi = lax.axis_index("gx")
    gj = lax.axis_index("gy")
    r = codes.shape[0]
    kv = codes.shape[1]
    heads = kv // HEAD
    nd = n // 2
    barrier = lax.optimization_barrier

    own = scaled(codes, scales)
    ra = r * 5 // 8 // 16 * 16
    shift = lambda x, s: lax.ppermute(x, "gx", [(i, (i + s) % n) for i in range(n)])
    flip = lambda x, mask: lax.ppermute(x, "gy", [(j, j ^ mask) for j in range(m)])
    part_a, part_b = own[:ra], own[ra:]
    near = [part_a] + [shift(part_a, s) for s in range(1, n)]
    far = [part_b] + [flip(part_b, s) for s in range(2, m, 2)]
    near, far = barrier((jnp.stack(near), jnp.stack(far)))
    near_all = [near] + [flip(near, s) for s in range(2, m, 2)]
    far_all = [far] + [shift(far, s) for s in range(1, n)]
    pieces = []
    for x in near_all + far_all:
        pieces += [x, flip(x, 1)]

    pm = signs(HEAD)
    had = jnp.asarray(pm, bf16)
    mean = jnp.asarray(block_mean_matrix(HEAD), bf16)
    side = jnp.where(gi < nd, 1, 0)
    where = jnp.stack([gi, gj, side]).astype(jnp.int32)
    keys, key_grad, qt, first0, weight = main_call(
        n, m, r, ra, where, tokens, gain.reshape(1, HEAD), cotangent, had, mean, pieces
    )

    hops = n - 1
    arrived = {}

    def hop(g, k, pay):
        arrived[g, k] = lax.ppermute(pay, "gx", [(g, g + 1), (n - 1 - g, n - 2 - g)])

    exchange = flip
    kept, met, parts, totals = {}, {}, {}, {}

    def phase_a(k):
        keep, send = recode_call(n, m, r, where, arrived[hops - 1, k], second[k], mean)
        kept[k] = keep
        met[k] = exchange(send, 1)

    def phase_b(k):
        whole = kept[k].astype(f32) + met[k].astype(f32)
        blocks = barrier(tuple([whole[0]] + [whole[x].astype(bf16) for x in range(1, m // 2)]))
        parts[k] = [blocks[0]]
        for x in range(1, m // 2):
            parts[k].append(exchange(blocks[x], 2 * x))

    def phase_c(k):
        total = parts[k][0]
        for x in parts[k][1:]:
            total = total + x.astype(f32)
        totals[k] = total

    def terms(is_first, skip, size):
        return list(term_call(n, m, r, where, tokens, qt, mean, is_first, skip, size))

    first = [first0] + terms(True, 1, 1) + terms(True, 2, heads - 2)
    second = terms(False, 0, heads)
    token_grad = None
    for part in range(TG_PARTS):
        token_grad = tgrad_call(key_grad, weight, token_grad, part, TG_PARTS)
    for k in range(heads):
        hop(0, k, first[k])
        for g in range(1, hops):
            hop(g, k, arrived[g - 1, k] + (first if g < nd else second)[k])
        phase_a(k)
        phase_b(k)
        phase_c(k)

    rotation = jnp.asarray(pm / np.float32(math.sqrt(HEAD)), f32)
    at_end = jnp.logical_or(gi == 0, gi == n - 1)
    out = []
    for batch in (list(range(heads - 1)), [heads - 1]):
        result = None
        for d in range(nd):
            value = jnp.stack([totals[k][d] for k in batch])
            if d == 0:
                value = jnp.where(at_end, value, 0.0)
            else:
                value = lax.ppermute(value.astype(bf16), "gx", [(0, d), (n - 1, n - 1 - d)]).astype(f32)
            result = value if result is None else result + value
        turned = jnp.einsum("har,ab->rhb", result, rotation, precision=HI)
        out.append(turned.reshape(r, len(batch) * HEAD))
    return keys, token_grad, jnp.concatenate(out, axis=1)


def solution(mesh):
    in_specs = (
        P(("gx", "gy"), None),
        P(("gx", "gy"), None),
        P(("gx", "gy"), None),
        P(),
        P(("gx", "gy"), None),
    )
    out_specs = (P(("gx", "gy"), None), P(("gx", "gy"), None), P(("gx", "gy"), None))

    return jax.shard_map(body, mesh=mesh, in_specs=in_specs, out_specs=out_specs, check_vma=False)
```

time: 266 us -> 205 us (0.77)
  waiting for transfers between devices: 139 us -> 69.3 us
  starting transfers between devices: 0.12 us -> 57 us
  Pallas kernels: 0 us -> 56.7 us
  local copies, waits for them, and re-layouts: 47.4 us -> 6.57 us
  matrix products: 37.1 us -> 0.64 us
  blocking collectives: 18 us -> 0 us
  between operations: 13.9 us -> 1.32 us
  other arithmetic: 9.49 us -> 12.5 us
    reduce_scatter x2 -> x0, waiting for transfers between devices: 103 us -> none  [the longest x1 76.9 us: body(): lax.psum_scatter(clipped(rotate(partial_value, rotation)).astype(jnp.bflo...]
    ppermute x0 -> x50, waiting for transfers between devices: none -> 69.3 us  [the longest x12 49 us: hop(): lax.ppermute(pay, 'gx', [(g, g + 1), (n - 1 - g, n - 2 - g)])]
    ppermute x0 -> x50, starting transfers between devices: none -> 57 us  [the longest x30 25.6 us: body(): lax.ppermute(x, 'gy', [(j, j ^ mask) for j in range(m)])]
    pallas_call x0 -> x13, Pallas kernels: none -> 56.7 us  [the longest x3 16.6 us: term_call(): pl.pallas_call(lambda *a: term_kernel(skip, *a), grid_spec=pltpu.Prefetch...]
    dot_general x5 -> x2, matrix products: 37.1 us -> 0.64 us  [body(): turned = jnp.einsum('har,ab->rhb', result, rotation, precision=HI)]
    all_gather x1 -> x0, waiting for transfers between devices: 36.4 us -> none  [collect(): gathered = lax.all_gather(near_rows, 'gy', axis=0, tiled=True)]
    dot_general x2 -> x0, local copies, waits for them, and re-layouts: 18.9 us -> none  [the longest x1 9.9 us: rotate(): jnp.einsum('rhc,cd->rhd', shaped, rotation, precision=lax.Precision.HIGHEST)]
    all_gather x1 -> x0, blocking collectives: 18 us -> none  [collect(): near_rows = lax.all_gather(pieces, 'gx', axis=0, tiled=True)]
  transfers between devices with their start and end apart: 3 -> 50, of which waited for: 3 -> 19; matrix products, arithmetic and copies ran while one was open for 5% -> 6% of each run, Pallas kernels for 0% -> 18%
where the time goes in v1:
time: 205 us; the launch traced here: 204 us
  waiting for transfers between devices  69.3 us (34%)
  starting transfers between devices  57 us (28%)
  Pallas kernels  56.7 us (28%)
  other arithmetic  12.5 us (6%)
  local copies, waits for them, and re-layouts  6.57 us (3%)
    ppermute x12, waiting for transfers between devices, hop(): lax.ppermute(pay, 'gx', [(g, g + 1), (n - 1 - g, n - 2 - g)])  49 us
    ppermute x30, starting transfers between devices, body(): lax.ppermute(x, 'gy', [(j, j ^ mask) for j in range(m)])  25.6 us
    ppermute x12, starting transfers between devices, hop(): lax.ppermute(pay, 'gx', [(g, g + 1), (n - 1 - g, n - 2 - g)])  17.2 us
    pallas_call x3, Pallas kernels, term_call(): pl.pallas_call(lambda *a: term_kernel(skip, *a), grid_spec=pltpu.Prefetch...  16.6 us
    pallas_call x4, Pallas kernels, tgrad_call(): pl.pallas_call(tgrad_kernel, grid=(steps,), in_specs=[pl.BlockSpec((tok,...  14.6 us
    pallas_call x1, Pallas kernels, main_call(): pl.pallas_call(lambda *a: main_kernel(n, m, r, ra, *a), out_shape=(jax.Sh...  13.9 us
    ppermute x6, waiting for transfers between devices, body(): lax.ppermute(x, 'gx', [(i, (i + s) % n) for i in range(n)])  13.3 us
    ppermute x6, starting transfers between devices, body(): lax.ppermute(x, 'gx', [(i, (i + s) % n) for i in range(n)])  11.6 us
  transfers between devices with their start and end apart: 50, of which 19 were waited for; matrix products, arithmetic and copies ran while one was open for 6% of the time, Pallas kernels for 18%

profile of v1, /device:TPU:0, one launch (start us, length us, event | category | flops | bytes accessed | tf_op | source)
XLA Modules:
  0.0 204.1 jit_solution(108014528223313448)
XLA Ops:
  0.6 1.6 scale_rows.1
  3.0 3.0 %collective-permute-start.4 = (bf16[48,512]{1,0:T(8,128)(2,1)S(1)}, bf16[48,512]{1,0:T(8,128)(2,1)S(1)}, u32[]{:S(2)}, u32[]{:S(2)}) collective-permute-start(bf16[48,512]{1,0:T(8,128)(2,1)S(1)} %get-tuple-element.98), channel_id=1, source_target_pairs={{0,4},{1,5},{2,6},{3,7},{4,0},{5,1},{6,2},{7,3},{8,12},{9,13},{10,... | collective-permute-start | bytes 147464 | tf_op jit(solution)/shard_map/ppermute | solution.py:301
  6.0 1.5 collective-permute-start.3
  7.6 0.9 slice_bitcast_fusion.17
  8.5 3.1 %collective-permute-start.1 = (bf16[80,512]{1,0:T(8,128)(2,1)S(1)}, bf16[80,512]{1,0:T(8,128)(2,1)S(1)}, u32[]{:S(2)}, u32[]{:S(2)}) collective-permute-start(bf16[80,512]{1,0:T(8,128)(2,1)S(1)} %get-tuple-element.100), channel_id=1, source_target_pairs={{0,16},{8,24},{16,0},{24,8},{1,17},{9,25},{17,1},{25,9},{2,18},{10... | collective-permute-start | bytes 245768 | tf_op jit(solution)/shard_map/ppermute | solution.py:300
  11.6 1.6 collective-permute-start
  13.1 2.2 %collective-permute-start.2 = (bf16[80,512]{1,0:T(8,128)(2,1)S(1)}, bf16[80,512]{1,0:T(8,128)(2,1)S(1)}, u32[]{:S(2)}, u32[]{:S(2)}) collective-permute-start(bf16[80,512]{1,0:T(8,128)(2,1)S(1)} %get-tuple-element.100), channel_id=1, source_target_pairs={{0,24},{8,0},{16,8},{24,16},{1,25},{9,1},{17,9},{25,17},{2,26},{10... | collective-permute-start | bytes 245768 | tf_op jit(solution)/shard_map/ppermute | solution.py:300
  16.3 1.8 collective-permute-done
  18.5 3.3 %collective-permute-start.18 = (bf16[4,48,512]{2,1,0:T(8,128)(2,1)S(1)}, bf16[4,48,512]{2,1,0:T(8,128)(2,1)S(1)}, u32[]{:S(2)}, u32[]{:S(2)}) collective-permute-start(bf16[4,48,512]{2,1,0:T(8,128)(2,1)S(1)} %pad_maximum_fusion.2.a_14_), channel_id=1, source_target_pairs={{0,24},{8,0},{16,8},{24,16},{1,25},{9,1},{17,9},{25,17},{2,26},{10... | collective-permute-start | bytes 589832 | tf_op jit(solution)/shard_map/ppermute | solution.py:300
  21.8 1.4 collective-permute-start.14
  23.2 2.4 %collective-permute-start.11 = (bf16[4,80,512]{2,1,0:T(8,128)(2,1)S(1)}, bf16[4,80,512]{2,1,0:T(8,128)(2,1)S(1)}, u32[]{:S(2)}, u32[]{:S(2)}) collective-permute-start(bf16[4,80,512]{2,1,0:T(8,128)(2,1)S(1)} %pad_maximum_fusion.a_6_), channel_id=1, source_target_pairs={{0,6},{1,7},{2,4},{3,5},{4,2},{5,3},{6,0},{7,1},{8,14},{9,15},{10,... | collective-permute-start | bytes 983048 | tf_op jit(solution)/shard_map/ppermute | solution.py:301
  26.2 1.0 collective-permute-done.18.a_20_
  27.1 1.5 collective-permute-start.7
  28.6 9.3 %collective-permute-done.16.a_18_ = bf16[4,48,512]{2,1,0:T(8,128)(2,1)S(1)} collective-permute-done((bf16[4,48,512]{2,1,0:T(8,128)(2,1)S(1)}, bf16[4,48,512]{2,1,0:T(8,128)(2,1)S(1)}, u32[]{:S(2)}, u32[]{:S(2)}) %collective-permute-start.16) | collective-permute-done | bytes 196640 | tf_op jit(solution)/shard_map/ppermute | solution.py:300
  38.5 0.9 collective-permute-done.13.a_15_
  44.4 13.9 %project.1 = (bf16[896,512]{1,0:T(8,128)(2,1)}, bf16[896,512]{1,0:T(8,128)(2,1)}, bf16[512,896]{1,0:T(8,128)(2,1)}, bf16[2,128,1024]{2,1,0:T(8,128)(2,1)}, bf16[4096,512]{1,0:T(8,128)(2,1)}) custom-call(s32[3]{0:T(128)} %pad_add_fusion.a_0_, bf16[896,4096]{1,0:T(8,128)(2,1)} %a_1_.7, f32[1,128]{1,0:T(1,128)} %bitcast.62, bf16[896,512]{1,0:T(8,128)(2,1)} %a_3_.8, ...), custom_call_target="tpu_custom_call" | custom-call | tf_op jit(solution)/shard_map/project/pallas_call | solution.py:159
  58.3 5.3 %terms.5 = (bf16[2,128,1024]{2,1,0:T(8,128)(2,1)}, bf16[2,128,1024]{2,1,0:T(8,128)(2,1)}) custom-call(s32[3]{0:T(128)} %pad_add_fusion.a_0_, bf16[896,4096]{1,0:T(8,128)(2,1)} %a_1_.7, bf16[512,896]{1,0:T(8,128)(2,1)} %get-tuple-element.46.a_2_, bf16[128,128]{1,0:T(8,128)(2,1)} %constant.25.clone.a_5_.a_3_), custom_call_target="tpu_custom_call" | custom-call | tf_op jit(solution)/shard_map/terms/pallas_call | solution.py:203
  63.6 4.5 %collective-permute-start.42 = (bf16[2,128,1024]{2,1,0:T(8,128)(2,1)}, bf16[2,128,1024]{2,1,0:T(8,128)(2,1)S(1)}, u32[]{:S(2)}, u32[]{:S(2)}) collective-permute-start(bf16[2,128,1024]{2,1,0:T(8,128)(2,1)} %get-tuple-element.69), channel_id=1, source_target_pairs={{0,8},{24,16},{1,9},{25,17},{2,10},{26,18},{3,11},{27,19},{4,12},{... | collective-permute-start | bytes 1572872 | tf_op jit(solution)/shard_map/ppermute | solution.py:325
  68.1 1.3 collective-permute-start.34
  69.4 4.5 %terms.4 = bf16[2,128,1024]{2,1,0:T(8,128)(2,1)} custom-call(s32[3]{0:T(128)} %pad_add_fusion.a_0_, bf16[896,4096]{1,0:T(8,128)(2,1)} %a_1_.7, bf16[512,896]{1,0:T(8,128)(2,1)} %get-tuple-element.46.a_2_, bf16[128,128]{1,0:T(8,128)(2,1)} %constant.25.clone.a_5_.a_3_), custom_call_target="tpu_custom_call" | custom-call | tf_op jit(solution)/shard_map/terms/pallas_call | solution.py:203
  74.0 1.3 collective-permute-start.27
  75.3 1.3 collective-permute-start.20
  76.6 4.0 %collective-permute-done.42 = bf16[2,128,1024]{2,1,0:T(8,128)(2,1)S(1)} collective-permute-done((bf16[2,128,1024]{2,1,0:T(8,128)(2,1)}, bf16[2,128,1024]{2,1,0:T(8,128)(2,1)S(1)}, u32[]{:S(2)}, u32[]{:S(2)}) %collective-permute-start.42) | collective-permute-done | bytes 524320 | tf_op jit(solution)/shard_map/ppermute | solution.py:325
  81.6 10.3 %collective-permute-done.34 = bf16[2,128,1024]{2,1,0:T(8,128)(2,1)S(1)} collective-permute-done((bf16[2,128,1024]{2,1,0:T(8,128)(2,1)}, bf16[2,128,1024]{2,1,0:T(8,128)(2,1)S(1)}, u32[]{:S(2)}, u32[]{:S(2)}) %collective-permute-start.34) | collective-permute-done | bytes 524320 | tf_op jit(solution)/shard_map/ppermute | solution.py:325
  92.8 10.3 %collective-permute-done.27 = bf16[2,128,1024]{2,1,0:T(8,128)(2,1)S(1)} collective-permute-done((bf16[2,128,1024]{2,1,0:T(8,128)(2,1)}, bf16[2,128,1024]{2,1,0:T(8,128)(2,1)S(1)}, u32[]{:S(2)}, u32[]{:S(2)}) %collective-permute-start.27) | collective-permute-done | bytes 524320 | tf_op jit(solution)/shard_map/ppermute | solution.py:325
  103.1 1.2 add.84
  104.4 1.5 collective-permute-start.28
  105.9 7.5 %collective-permute-done.20 = bf16[2,128,1024]{2,1,0:T(8,128)(2,1)S(1)} collective-permute-done((bf16[2,128,1024]{2,1,0:T(8,128)(2,1)S(1)}, bf16[2,128,1024]{2,1,0:T(8,128)(2,1)S(1)}, u32[]{:S(2)}, u32[]{:S(2)}) %collective-permute-start.20) | collective-permute-done | bytes 524320 | tf_op jit(solution)/shard_map/ppermute | solution.py:325
  114.3 6.8 %terms.3 = (bf16[2,128,1024]{2,1,0:T(8,128)(2,1)}, bf16[2,128,1024]{2,1,0:T(8,128)(2,1)}, bf16[2,128,1024]{2,1,0:T(8,128)(2,1)}, bf16[2,128,1024]{2,1,0:T(8,128)(2,1)}) custom-call(s32[3]{0:T(128)} %pad_add_fusion.a_0_, bf16[896,4096]{1,0:T(8,128)(2,1)} %a_1_.7, bf16[512,896]{1,0:T(8,128)(2,1)} %get-tuple-element.46.a_2_, ...), custom_call_target="tpu_custom_call" | custom-call | tf_op jit(solution)/shard_map/terms/pallas_call | solution.py:203
  121.1 1.2 add.98
  122.3 1.3 collective-permute-start.44
  123.7 1.2 add.91
  124.9 1.3 collective-permute-start.36
  126.2 1.4 add.85
  127.6 1.3 collective-permute-start.29
  128.9 1.2 add.79
  130.2 1.3 collective-permute-start.22
  131.5 8.8 %collective-permute-done.44.a_1_ = bf16[2,128,1024]{2,1,0:T(8,128)(2,1)} collective-permute-done((bf16[2,128,1024]{2,1,0:T(8,128)(2,1)S(1)}, bf16[2,128,1024]{2,1,0:T(8,128)(2,1)}, u32[]{:S(2)}, u32[]{:S(2)}) %collective-permute-start.44) | collective-permute-done | bytes 524320 | tf_op jit(solution)/shard_map/ppermute | solution.py:325
  140.2 2.6 %recode.7 = (bf16[4,2,128,128]{3,2,1,0:T(8,128)(2,1)}, bf16[4,2,128,128]{3,2,1,0:T(8,128)(2,1)}) custom-call(s32[3]{0:T(128)} %pad_add_fusion.a_0_, bf16[2,128,1024]{2,1,0:T(8,128)(2,1)} %collective-permute-done.44.a_1_, bf16[2,128,1024]{2,1,0:T(8,128)(2,1)} %get-tuple-element.70.a_2_, bf16[128,128]{1,0:T(8,128)(2,1)} %constant.25.clone.a_5_.a_3_), custom_call_target="tpu_custom_call" | custom-call | tf_op jit(solution)/shard_map/recode/pallas_call | solution.py:271
  142.9 3.6 %token_grad.4.refs_0_ = bf16[896,4096]{1,0:T(8,128)(2,1)} custom-call(bf16[896,512]{1,0:T(8,128)(2,1)} %get-tuple-element.43.kg_ref, bf16[4096,512]{1,0:T(8,128)(2,1)} %get-tuple-element.44.w_ref), custom_call_target="tpu_custom_call" | custom-call | tf_op jit(solution)/shard_map/token_grad/pallas_call | solution.py:234
  146.5 3.6 %token_grad.5.refs_0_ = bf16[896,4096]{1,0:T(8,128)(2,1)} custom-call(bf16[896,512]{1,0:T(8,128)(2,1)} %get-tuple-element.43.kg_ref, bf16[4096,512]{1,0:T(8,128)(2,1)} %get-tuple-element.44.w_ref, bf16[896,4096]{1,0:T(8,128)(2,1)} %token_grad.4.refs_0_), custom_call_target="tpu_custom_call", output_to_operand_aliasing={{}: (2, {})} | custom-call | tf_op jit(solution)/shard_map/token_grad/pallas_call | solution.py:234
  150.1 3.6 %token_grad.6.refs_0_ = bf16[896,4096]{1,0:T(8,128)(2,1)} custom-call(bf16[896,512]{1,0:T(8,128)(2,1)} %get-tuple-element.43.kg_ref, bf16[4096,512]{1,0:T(8,128)(2,1)} %get-tuple-element.44.w_ref, bf16[896,4096]{1,0:T(8,128)(2,1)} %token_grad.5.refs_0_), custom_call_target="tpu_custom_call", output_to_operand_aliasing={{}: (2, {})} | custom-call | tf_op jit(solution)/shard_map/token_grad/pallas_call | solution.py:234
  153.8 3.7 %token_grad.7 = bf16[896,4096]{1,0:T(8,128)(2,1)} custom-call(bf16[896,512]{1,0:T(8,128)(2,1)} %get-tuple-element.43.kg_ref, bf16[4096,512]{1,0:T(8,128)(2,1)} %get-tuple-element.44.w_ref, bf16[896,4096]{1,0:T(8,128)(2,1)} %token_grad.6.refs_0_), custom_call_target="tpu_custom_call", output_to_operand_aliasing={{}: (2, {})} | custom-call | tf_op jit(solution)/shard_map/token_grad/pallas_call | solution.py:234
  158.2 2.5 %recode.6 = (bf16[4,2,128,128]{3,2,1,0:T(8,128)(2,1)}, bf16[4,2,128,128]{3,2,1,0:T(8,128)(2,1)}) custom-call(s32[3]{0:T(128)} %pad_add_fusion.a_0_, bf16[2,128,1024]{2,1,0:T(8,128)(2,1)} %copy-done.7, bf16[2,128,1024]{2,1,0:T(8,128)(2,1)} %get-tuple-element.62.a_2_, bf16[128,128]{1,0:T(8,128)(2,1)} %constant.25.clone.a_5_.a_3_), custom_call_target="tpu_custom_call" | custom-call | tf_op jit(solution)/shard_map/recode/pallas_call | solution.py:271
  161.2 1.3 collective-permute-done.29.a_1_
  163.4 2.5 %recode.5 = (bf16[4,2,128,128]{3,2,1,0:T(8,128)(2,1)}, bf16[4,2,128,128]{3,2,1,0:T(8,128)(2,1)}) custom-call(s32[3]{0:T(128)} %pad_add_fusion.a_0_, bf16[2,128,1024]{2,1,0:T(8,128)(2,1)} %copy-done.6, bf16[2,128,1024]{2,1,0:T(8,128)(2,1)} %get-tuple-element.54.a_2_, bf16[128,128]{1,0:T(8,128)(2,1)} %constant.25.clone.a_5_.a_3_), custom_call_target="tpu_custom_call" | custom-call | tf_op jit(solution)/shard_map/recode/pallas_call | solution.py:271
  165.9 6.7 %collective-permute-done.22.a_1_ = bf16[2,128,1024]{2,1,0:T(8,128)(2,1)S(1)} collective-permute-done((bf16[2,128,1024]{2,1,0:T(8,128)(2,1)S(1)}, bf16[2,128,1024]{2,1,0:T(8,128)(2,1)S(1)}, u32[]{:S(2)}, u32[]{:S(2)}) %collective-permute-start.22) | collective-permute-done | bytes 524320 | tf_op jit(solution)/shard_map/ppermute | solution.py:325
  173.3 2.5 %recode.4 = (bf16[4,2,128,128]{3,2,1,0:T(8,128)(2,1)}, bf16[4,2,128,128]{3,2,1,0:T(8,128)(2,1)}) custom-call(s32[3]{0:T(128)} %pad_add_fusion.a_0_, bf16[2,128,1024]{2,1,0:T(8,128)(2,1)} %copy-done.5, bf16[2,128,1024]{2,1,0:T(8,128)(2,1)} %get-tuple-element.47.a_2_, bf16[128,128]{1,0:T(8,128)(2,1)} %constant.25.clone.a_5_.a_3_), custom_call_target="tpu_custom_call" | custom-call | tf_op jit(solution)/shard_map/recode/pallas_call | solution.py:271
  175.8 1.0 fusion.23
  176.9 1.6 collective-permute-start.46
  178.4 1.5 collective-permute-start.47
  180.4 1.0 fusion.22
  181.5 1.6 collective-permute-start.38
  183.1 1.0 fusion.21
  184.2 1.6 collective-permute-start.39
  185.7 1.0 fusion.20
  187.4 1.5 collective-permute-start.31
  188.9 1.5 collective-permute-start.32
  191.0 1.5 collective-permute-start.24
  192.5 1.5 collective-permute-start.25
  194.6 1.3 collective-permute-start.49
  197.1 2.2 %collective-permute-done.26 = bf16[2,128,128]{2,1,0:T(8,128)(2,1)S(1)} collective-permute-done((bf16[2,128,128]{2,1,0:T(8,128)(2,1)S(1)}, bf16[2,128,128]{2,1,0:T(8,128)(2,1)S(1)}, u32[]{:S(2)}, u32[]{:S(2)}) %collective-permute-start.26) | collective-permute-done | bytes 65568 | tf_op jit(solution)/shard_map/ppermute | solution.py:301
  199.4 1.3 collective-permute-start.41
  201.0 1.9 collective-permute-done.41
  (136 shorter events, 18.8 us)
Async XLA Ops:
  3.0 10.1 %collective-permute-start.4 = (bf16[48,512]{1,0:T(8,128)(2,1)S(1)}, bf16[48,512]{1,0:T(8,128)(2,1)S(1)}, u32[]{:S(2)}, u32[]{:S(2)}) collective-permute-start(bf16[48,512]{1,0:T(8,128)(2,1)S(1)} %get-tuple-element.98), channel_id=1, source_target_pairs={{0,4},{1,5},{2,6},{3,7},{4,0},{5,1},{6,2},{7,3},{8,12},{9,13},{10,... | collective-permute-start | bytes 147464 | tf_op jit(solution)/shard_map/ppermute | solution.py:301
  6.0 9.4 %collective-permute-start.3 = (bf16[48,512]{1,0:T(8,128)(2,1)S(1)}, bf16[48,512]{1,0:T(8,128)(2,1)S(1)}, u32[]{:S(2)}, u32[]{:S(2)}) collective-permute-start(bf16[48,512]{1,0:T(8,128)(2,1)S(1)} %get-tuple-element.98), channel_id=1, source_target_pairs={{0,2},{1,3},{2,0},{3,1},{4,6},{5,7},{6,4},{7,5},{8,10},{9,11},{10,... | collective-permute-start | bytes 147464 | tf_op jit(solution)/shard_map/ppermute | solution.py:301
  7.5 7.9 %collective-permute-start.5 = (bf16[48,512]{1,0:T(8,128)(2,1)S(1)}, bf16[48,512]{1,0:T(8,128)(2,1)S(1)}, u32[]{:S(2)}, u32[]{:S(2)}) collective-permute-start(bf16[48,512]{1,0:T(8,128)(2,1)S(1)} %get-tuple-element.98), channel_id=1, source_target_pairs={{0,6},{1,7},{2,4},{3,5},{4,2},{5,3},{6,0},{7,1},{8,14},{9,15},{10,... | collective-permute-start | bytes 147464 | tf_op jit(solution)/shard_map/ppermute | solution.py:301
  8.5 7.8 %collective-permute-start.1 = (bf16[80,512]{1,0:T(8,128)(2,1)S(1)}, bf16[80,512]{1,0:T(8,128)(2,1)S(1)}, u32[]{:S(2)}, u32[]{:S(2)}) collective-permute-start(bf16[80,512]{1,0:T(8,128)(2,1)S(1)} %get-tuple-element.100), channel_id=1, source_target_pairs={{0,16},{8,24},{16,0},{24,8},{1,17},{9,25},{17,1},{25,9},{2,18},{10... | collective-permute-start | bytes 245768 | tf_op jit(solution)/shard_map/ppermute | solution.py:300
  11.6 6.5 %collective-permute-start = (bf16[80,512]{1,0:T(8,128)(2,1)S(1)}, bf16[80,512]{1,0:T(8,128)(2,1)S(1)}, u32[]{:S(2)}, u32[]{:S(2)}) collective-permute-start(bf16[80,512]{1,0:T(8,128)(2,1)S(1)} %get-tuple-element.100), channel_id=1, source_target_pairs={{0,8},{8,16},{16,24},{24,0},{1,9},{9,17},{17,25},{25,1},{2,10},{10... | collective-permute-start | bytes 245768 | tf_op jit(solution)/shard_map/ppermute | solution.py:300
  13.1 5.3 %collective-permute-start.2 = (bf16[80,512]{1,0:T(8,128)(2,1)S(1)}, bf16[80,512]{1,0:T(8,128)(2,1)S(1)}, u32[]{:S(2)}, u32[]{:S(2)}) collective-permute-start(bf16[80,512]{1,0:T(8,128)(2,1)S(1)} %get-tuple-element.100), channel_id=1, source_target_pairs={{0,24},{8,0},{16,8},{24,16},{1,25},{9,1},{17,9},{25,17},{2,26},{10... | collective-permute-start | bytes 245768 | tf_op jit(solution)/shard_map/ppermute | solution.py:300
  15.4 28.0 %copy-start.1 = (bf16[4,48,512]{2,1,0:T(8,128)(2,1)}, bf16[4,48,512]{2,1,0:T(8,128)(2,1)S(1)}, u32[]{:S(2)}) copy-start(bf16[4,48,512]{2,1,0:T(8,128)(2,1)S(1)} %pad_maximum_fusion.2.a_14_) | copy-start | bytes 589828
  18.5 24.9 %copy-start = (bf16[4,80,512]{2,1,0:T(8,128)(2,1)}, bf16[4,80,512]{2,1,0:T(8,128)(2,1)S(1)}, u32[]{:S(2)}) copy-start(bf16[4,80,512]{2,1,0:T(8,128)(2,1)S(1)} %pad_maximum_fusion.a_6_) | copy-start | bytes 983044
  18.5 8.6 %collective-permute-start.18 = (bf16[4,48,512]{2,1,0:T(8,128)(2,1)S(1)}, bf16[4,48,512]{2,1,0:T(8,128)(2,1)S(1)}, u32[]{:S(2)}, u32[]{:S(2)}) collective-permute-start(bf16[4,48,512]{2,1,0:T(8,128)(2,1)S(1)} %pad_maximum_fusion.2.a_14_), channel_id=1, source_target_pairs={{0,24},{8,0},{16,8},{24,16},{1,25},{9,1},{17,9},{25,17},{2,26},{10... | collective-permute-start | bytes 589832 | tf_op jit(solution)/shard_map/ppermute | solution.py:300
  21.8 16.1 %collective-permute-start.16 = (bf16[4,48,512]{2,1,0:T(8,128)(2,1)S(1)}, bf16[4,48,512]{2,1,0:T(8,128)(2,1)S(1)}, u32[]{:S(2)}, u32[]{:S(2)}) collective-permute-start(bf16[4,48,512]{2,1,0:T(8,128)(2,1)S(1)} %pad_maximum_fusion.2.a_14_), channel_id=1, source_target_pairs={{0,16},{8,24},{16,0},{24,8},{1,17},{9,25},{17,1},{25,9},{2,18},{10... | collective-permute-start | bytes 589832 | tf_op jit(solution)/shard_map/ppermute | solution.py:300
  21.8 16.1 %collective-permute-start.14 = (bf16[4,48,512]{2,1,0:T(8,128)(2,1)S(1)}, bf16[4,48,512]{2,1,0:T(8,128)(2,1)S(1)}, u32[]{:S(2)}, u32[]{:S(2)}) collective-permute-start(bf16[4,48,512]{2,1,0:T(8,128)(2,1)S(1)} %pad_maximum_fusion.2.a_14_), channel_id=1, source_target_pairs={{0,8},{8,16},{16,24},{24,0},{1,9},{9,17},{17,25},{25,1},{2,10},{10... | collective-permute-start | bytes 589832 | tf_op jit(solution)/shard_map/ppermute | solution.py:300
  23.2 16.9 %collective-permute-start.11 = (bf16[4,80,512]{2,1,0:T(8,128)(2,1)S(1)}, bf16[4,80,512]{2,1,0:T(8,128)(2,1)S(1)}, u32[]{:S(2)}, u32[]{:S(2)}) collective-permute-start(bf16[4,80,512]{2,1,0:T(8,128)(2,1)S(1)} %pad_maximum_fusion.a_6_), channel_id=1, source_target_pairs={{0,6},{1,7},{2,4},{3,5},{4,2},{5,3},{6,0},{7,1},{8,14},{9,15},{10,... | collective-permute-start | bytes 983048 | tf_op jit(solution)/shard_map/ppermute | solution.py:301
  25.7 14.6 %collective-permute-start.9 = (bf16[4,80,512]{2,1,0:T(8,128)(2,1)S(1)}, bf16[4,80,512]{2,1,0:T(8,128)(2,1)S(1)}, u32[]{:S(2)}, u32[]{:S(2)}) collective-permute-start(bf16[4,80,512]{2,1,0:T(8,128)(2,1)S(1)} %pad_maximum_fusion.a_6_), channel_id=1, source_target_pairs={{0,4},{1,5},{2,6},{3,7},{4,0},{5,1},{6,2},{7,3},{8,12},{9,13},{10,... | collective-permute-start | bytes 983048 | tf_op jit(solution)/shard_map/ppermute | solution.py:301
  27.1 16.3 %copy-start.16 = (bf16[4,48,512]{2,1,0:T(8,128)(2,1)}, bf16[4,48,512]{2,1,0:T(8,128)(2,1)S(1)}, u32[]{:S(2)}) copy-start(bf16[4,48,512]{2,1,0:T(8,128)(2,1)S(1)} %collective-permute-done.18.a_20_) | copy-start | bytes 589828
  27.1 13.5 %collective-permute-start.7 = (bf16[4,80,512]{2,1,0:T(8,128)(2,1)S(1)}, bf16[4,80,512]{2,1,0:T(8,128)(2,1)S(1)}, u32[]{:S(2)}, u32[]{:S(2)}) collective-permute-start(bf16[4,80,512]{2,1,0:T(8,128)(2,1)S(1)} %pad_maximum_fusion.a_6_), channel_id=1, source_target_pairs={{0,2},{1,3},{2,0},{3,1},{4,6},{5,7},{6,4},{7,5},{8,10},{9,11},{10,... | collective-permute-start | bytes 983048 | tf_op jit(solution)/shard_map/ppermute | solution.py:301
  37.9 5.5 %copy-start.17 = (bf16[4,48,512]{2,1,0:T(8,128)(2,1)}, bf16[4,48,512]{2,1,0:T(8,128)(2,1)S(1)}, u32[]{:S(2)}) copy-start(bf16[4,48,512]{2,1,0:T(8,128)(2,1)S(1)} %collective-permute-done.16.a_18_) | copy-start | bytes 589828
  37.9 1.4 collective-permute-start.13
  38.0 5.5 %copy-start.18 = (bf16[4,48,512]{2,1,0:T(8,128)(2,1)}, bf16[4,48,512]{2,1,0:T(8,128)(2,1)S(1)}, u32[]{:S(2)}) copy-start(bf16[4,48,512]{2,1,0:T(8,128)(2,1)S(1)} %collective-permute-done.14.a_16_) | copy-start | bytes 589828
  38.0 2.8 %collective-permute-start.6 = (bf16[4,80,512]{2,1,0:T(8,128)(2,1)S(1)}, bf16[4,80,512]{2,1,0:T(8,128)(2,1)S(1)}, u32[]{:S(2)}, u32[]{:S(2)}) collective-permute-start(bf16[4,80,512]{2,1,0:T(8,128)(2,1)S(1)} %pad_maximum_fusion.a_6_), channel_id=1, source_target_pairs={{0,1},{1,0},{2,3},{3,2},{4,5},{5,4},{6,7},{7,6},{8,9},{9,8},{10,11... | collective-permute-start | bytes 983048 | tf_op jit(solution)/shard_map/ppermute | solution.py:301
  39.4 1.7 collective-permute-start.19
  40.1 3.4 %copy-start.8 = (bf16[4,80,512]{2,1,0:T(8,128)(2,1)}, bf16[4,80,512]{2,1,0:T(8,128)(2,1)S(1)}, u32[]{:S(2)}) copy-start(bf16[4,80,512]{2,1,0:T(8,128)(2,1)S(1)} %collective-permute-done.11.a_12_) | copy-start | bytes 983044
  40.1 3.3 %collective-permute-start.12 = (bf16[4,80,512]{2,1,0:T(8,128)(2,1)S(1)}, bf16[4,80,512]{2,1,0:T(8,128)(2,1)S(1)}, u32[]{:S(2)}, u32[]{:S(2)}) collective-permute-start(bf16[4,80,512]{2,1,0:T(8,128)(2,1)S(1)} %collective-permute-done.11.a_12_), channel_id=1, source_target_pairs={{0,1},{1,0},{2,3},{3,2},{4,5},{5,4},{6,7},{7,6},{8,9},{9,8},{10,11... | collective-permute-start | bytes 983048 | tf_op jit(solution)/shard_map/ppermute | solution.py:301
  40.2 3.2 %copy-start.9 = (bf16[4,80,512]{2,1,0:T(8,128)(2,1)}, bf16[4,80,512]{2,1,0:T(8,128)(2,1)S(1)}, u32[]{:S(2)}) copy-start(bf16[4,80,512]{2,1,0:T(8,128)(2,1)S(1)} %collective-permute-done.9.a_10_) | copy-start | bytes 983044
  40.2 3.2 %collective-permute-start.10 = (bf16[4,80,512]{2,1,0:T(8,128)(2,1)S(1)}, bf16[4,80,512]{2,1,0:T(8,128)(2,1)S(1)}, u32[]{:S(2)}, u32[]{:S(2)}) collective-permute-start(bf16[4,80,512]{2,1,0:T(8,128)(2,1)S(1)} %collective-permute-done.9.a_10_), channel_id=1, source_target_pairs={{0,1},{1,0},{2,3},{3,2},{4,5},{5,4},{6,7},{7,6},{8,9},{9,8},{10,11... | collective-permute-start | bytes 983048 | tf_op jit(solution)/shard_map/ppermute | solution.py:301
  40.6 2.9 %copy-start.10 = (bf16[4,80,512]{2,1,0:T(8,128)(2,1)}, bf16[4,80,512]{2,1,0:T(8,128)(2,1)S(1)}, u32[]{:S(2)}) copy-start(bf16[4,80,512]{2,1,0:T(8,128)(2,1)S(1)} %collective-permute-done.7.a_8_) | copy-start | bytes 983044
  40.6 2.8 %collective-permute-start.8 = (bf16[4,80,512]{2,1,0:T(8,128)(2,1)S(1)}, bf16[4,80,512]{2,1,0:T(8,128)(2,1)S(1)}, u32[]{:S(2)}, u32[]{:S(2)}) collective-permute-start(bf16[4,80,512]{2,1,0:T(8,128)(2,1)S(1)} %collective-permute-done.7.a_8_), channel_id=1, source_target_pairs={{0,1},{1,0},{2,3},{3,2},{4,5},{5,4},{6,7},{7,6},{8,9},{9,8},{10,11... | collective-permute-start | bytes 983048 | tf_op jit(solution)/shard_map/ppermute | solution.py:301
  40.7 2.3 %collective-permute-start.17 = (bf16[4,48,512]{2,1,0:T(8,128)(2,1)S(1)}, bf16[4,48,512]{2,1,0:T(8,128)(2,1)}, u32[]{:S(2)}, u32[]{:S(2)}) collective-permute-start(bf16[4,48,512]{2,1,0:T(8,128)(2,1)S(1)} %collective-permute-done.16.a_18_), channel_id=1, source_target_pairs={{0,1},{1,0},{2,3},{3,2},{4,5},{5,4},{6,7},{7,6},{8,9},{9,8},{10,11... | collective-permute-start | bytes 589832 | tf_op jit(solution)/shard_map/ppermute | solution.py:301
  41.8 1.6 collective-permute-start.15
  58.3 17.0 %copy-start.2 = (bf16[2,128,1024]{2,1,0:T(8,128)(2,1)S(1)}, bf16[2,128,1024]{2,1,0:T(8,128)(2,1)}, u32[]{:S(2)}) copy-start(bf16[2,128,1024]{2,1,0:T(8,128)(2,1)} %get-tuple-element.45) | copy-start | bytes 1572868
  63.6 17.1 %copy-start.4 = (bf16[2,128,1024]{2,1,0:T(8,128)(2,1)S(1)}, bf16[2,128,1024]{2,1,0:T(8,128)(2,1)}, u32[]{:S(2)}) copy-start(bf16[2,128,1024]{2,1,0:T(8,128)(2,1)} %get-tuple-element.69) | copy-start | bytes 1572868
  63.6 28.3 %copy-start.3 = (bf16[2,128,1024]{2,1,0:T(8,128)(2,1)S(1)}, bf16[2,128,1024]{2,1,0:T(8,128)(2,1)}, u32[]{:S(2)}) copy-start(bf16[2,128,1024]{2,1,0:T(8,128)(2,1)} %get-tuple-element.61) | copy-start | bytes 1572868
  63.6 17.0 %collective-permute-start.42 = (bf16[2,128,1024]{2,1,0:T(8,128)(2,1)}, bf16[2,128,1024]{2,1,0:T(8,128)(2,1)S(1)}, u32[]{:S(2)}, u32[]{:S(2)}) collective-permute-start(bf16[2,128,1024]{2,1,0:T(8,128)(2,1)} %get-tuple-element.69), channel_id=1, source_target_pairs={{0,8},{24,16},{1,9},{25,17},{2,10},{26,18},{3,11},{27,19},{4,12},{... | collective-permute-start | bytes 1572872 | tf_op jit(solution)/shard_map/ppermute | solution.py:325
  68.1 23.8 %collective-permute-start.34 = (bf16[2,128,1024]{2,1,0:T(8,128)(2,1)}, bf16[2,128,1024]{2,1,0:T(8,128)(2,1)S(1)}, u32[]{:S(2)}, u32[]{:S(2)}) collective-permute-start(bf16[2,128,1024]{2,1,0:T(8,128)(2,1)} %get-tuple-element.61), channel_id=1, source_target_pairs={{0,8},{24,16},{1,9},{25,17},{2,10},{26,18},{3,11},{27,19},{4,12},{... | collective-permute-start | bytes 1572872 | tf_op jit(solution)/shard_map/ppermute | solution.py:325
  74.0 29.2 %collective-permute-start.27 = (bf16[2,128,1024]{2,1,0:T(8,128)(2,1)}, bf16[2,128,1024]{2,1,0:T(8,128)(2,1)S(1)}, u32[]{:S(2)}, u32[]{:S(2)}) collective-permute-start(bf16[2,128,1024]{2,1,0:T(8,128)(2,1)} %terms.4), channel_id=1, source_target_pairs={{0,8},{24,16},{1,9},{25,17},{2,10},{26,18},{3,11},{27,19},{4,12},{... | collective-permute-start | bytes 1572872 | tf_op jit(solution)/shard_map/ppermute | solution.py:325
  75.3 38.2 %collective-permute-start.20 = (bf16[2,128,1024]{2,1,0:T(8,128)(2,1)S(1)}, bf16[2,128,1024]{2,1,0:T(8,128)(2,1)S(1)}, u32[]{:S(2)}, u32[]{:S(2)}) collective-permute-start(bf16[2,128,1024]{2,1,0:T(8,128)(2,1)S(1)} %copy-done.2), channel_id=1, source_target_pairs={{0,8},{24,16},{1,9},{25,17},{2,10},{26,18},{3,11},{27,19},{4,12},{... | collective-permute-start | bytes 1572872 | tf_op jit(solution)/shard_map/ppermute | solution.py:325
  80.9 40.2 %collective-permute-start.43 = (bf16[2,128,1024]{2,1,0:T(8,128)(2,1)S(1)}, bf16[2,128,1024]{2,1,0:T(8,128)(2,1)S(1)}, u32[]{:S(2)}, u32[]{:S(2)}) collective-permute-start(bf16[2,128,1024]{2,1,0:T(8,128)(2,1)S(1)} %add.97), channel_id=1, source_target_pairs={{8,16},{16,8},{9,17},{17,9},{10,18},{18,10},{11,19},{19,11},{12,20... | collective-permute-start | bytes 1572872 | tf_op jit(solution)/shard_map/ppermute | solution.py:325
  92.1 31.5 %collective-permute-start.35 = (bf16[2,128,1024]{2,1,0:T(8,128)(2,1)S(1)}, bf16[2,128,1024]{2,1,0:T(8,128)(2,1)S(1)}, u32[]{:S(2)}, u32[]{:S(2)}) collective-permute-start(bf16[2,128,1024]{2,1,0:T(8,128)(2,1)S(1)} %add.90), channel_id=1, source_target_pairs={{8,16},{16,8},{9,17},{17,9},{10,18},{18,10},{11,19},{19,11},{12,20... | collective-permute-start | bytes 1572872 | tf_op jit(solution)/shard_map/ppermute | solution.py:325
  104.4 21.8 %collective-permute-start.28 = (bf16[2,128,1024]{2,1,0:T(8,128)(2,1)S(1)}, bf16[2,128,1024]{2,1,0:T(8,128)(2,1)}, u32[]{:S(2)}, u32[]{:S(2)}) collective-permute-start(bf16[2,128,1024]{2,1,0:T(8,128)(2,1)S(1)} %add.84), channel_id=1, source_target_pairs={{8,16},{16,8},{9,17},{17,9},{10,18},{18,10},{11,19},{19,11},{12,20... | collective-permute-start | bytes 1572872 | tf_op jit(solution)/shard_map/ppermute | solution.py:325
  113.6 15.3 %collective-permute-start.21 = (bf16[2,128,1024]{2,1,0:T(8,128)(2,1)S(1)}, bf16[2,128,1024]{2,1,0:T(8,128)(2,1)S(1)}, u32[]{:S(2)}, u32[]{:S(2)}) collective-permute-start(bf16[2,128,1024]{2,1,0:T(8,128)(2,1)S(1)} %add.78), channel_id=1, source_target_pairs={{8,16},{16,8},{9,17},{17,9},{10,18},{18,10},{11,19},{19,11},{12,20... | collective-permute-start | bytes 1572872 | tf_op jit(solution)/shard_map/ppermute | solution.py:325
  122.3 17.9 %collective-permute-start.44 = (bf16[2,128,1024]{2,1,0:T(8,128)(2,1)S(1)}, bf16[2,128,1024]{2,1,0:T(8,128)(2,1)}, u32[]{:S(2)}, u32[]{:S(2)}) collective-permute-start(bf16[2,128,1024]{2,1,0:T(8,128)(2,1)S(1)} %add.98), channel_id=1, source_target_pairs={{16,24},{8,0},{17,25},{9,1},{18,26},{10,2},{19,27},{11,3},{20,28},... | collective-permute-start | bytes 1572872 | tf_op jit(solution)/shard_map/ppermute | solution.py:325
  124.9 32.5 %collective-permute-start.36 = (bf16[2,128,1024]{2,1,0:T(8,128)(2,1)S(1)}, bf16[2,128,1024]{2,1,0:T(8,128)(2,1)S(1)}, u32[]{:S(2)}, u32[]{:S(2)}) collective-permute-start(bf16[2,128,1024]{2,1,0:T(8,128)(2,1)S(1)} %add.91), channel_id=1, source_target_pairs={{16,24},{8,0},{17,25},{9,1},{18,26},{10,2},{19,27},{11,3},{20,28},... | collective-permute-start | bytes 1572872 | tf_op jit(solution)/shard_map/ppermute | solution.py:325
  127.6 35.0 %collective-permute-start.29 = (bf16[2,128,1024]{2,1,0:T(8,128)(2,1)S(1)}, bf16[2,128,1024]{2,1,0:T(8,128)(2,1)S(1)}, u32[]{:S(2)}, u32[]{:S(2)}) collective-permute-start(bf16[2,128,1024]{2,1,0:T(8,128)(2,1)S(1)} %add.85), channel_id=1, source_target_pairs={{16,24},{8,0},{17,25},{9,1},{18,26},{10,2},{19,27},{11,3},{20,28},... | collective-permute-start | bytes 1572872 | tf_op jit(solution)/shard_map/ppermute | solution.py:325
  130.2 42.4 %collective-permute-start.22 = (bf16[2,128,1024]{2,1,0:T(8,128)(2,1)S(1)}, bf16[2,128,1024]{2,1,0:T(8,128)(2,1)S(1)}, u32[]{:S(2)}, u32[]{:S(2)}) collective-permute-start(bf16[2,128,1024]{2,1,0:T(8,128)(2,1)S(1)} %add.79), channel_id=1, source_target_pairs={{16,24},{8,0},{17,25},{9,1},{18,26},{10,2},{19,27},{11,3},{20,28},... | collective-permute-start | bytes 1572872 | tf_op jit(solution)/shard_map/ppermute | solution.py:325
  142.9 32.9 %collective-permute-start.45 = (bf16[4,2,128,128]{3,2,1,0:T(8,128)(2,1)}, bf16[4,2,128,128]{3,2,1,0:T(8,128)(2,1)}, u32[]{:S(2)}, u32[]{:S(2)}) collective-permute-start(bf16[4,2,128,128]{3,2,1,0:T(8,128)(2,1)} %get-tuple-element.72), channel_id=1, source_target_pairs={{0,1},{1,0},{2,3},{3,2},{4,5},{5,4},{6,7},{7,6},{8,9},{9,8},{10,11... | collective-permute-start | bytes 786440 | tf_op jit(solution)/shard_map/ppermute | solution.py:301
  153.8 22.0 %copy-start.15 = (bf16[4,2,128,128]{3,2,1,0:T(8,128)(2,1)S(1)}, bf16[4,2,128,128]{3,2,1,0:T(8,128)(2,1)}, u32[]{:S(2)}) copy-start(bf16[4,2,128,128]{3,2,1,0:T(8,128)(2,1)} %get-tuple-element.71) | copy-start | bytes 786436
  157.4 43.3 %copy-start.22 = (f32[128,128]{0,1:T(8,128)S(1)}, f32[128,128]{0,1:T(8,128)}, u32[]{:S(2)}) copy-start(f32[128,128]{0,1:T(8,128)} %constant.26.clone) | copy-start | bytes 196612
  157.4 45.5 %copy-start.21 = (f32[128,128,1]{0,1,2:T(8,128)S(1)}, f32[128,128,1]{0,1,2:T(8,128)}, u32[]{:S(2)}) copy-start(f32[128,128,1]{0,1,2:T(8,128)} %constant.28) | copy-start | bytes 196612
  160.7 19.2 %collective-permute-start.37 = (bf16[4,2,128,128]{3,2,1,0:T(8,128)(2,1)}, bf16[4,2,128,128]{3,2,1,0:T(8,128)(2,1)S(1)}, u32[]{:S(2)}, u32[]{:S(2)}) collective-permute-start(bf16[4,2,128,128]{3,2,1,0:T(8,128)(2,1)} %get-tuple-element.64), channel_id=1, source_target_pairs={{0,1},{1,0},{2,3},{3,2},{4,5},{5,4},{6,7},{7,6},{8,9},{9,8},{10,11... | collective-permute-start | bytes 786440 | tf_op jit(solution)/shard_map/ppermute | solution.py:301
  165.9 15.7 %collective-permute-start.30 = (bf16[4,2,128,128]{3,2,1,0:T(8,128)(2,1)}, bf16[4,2,128,128]{3,2,1,0:T(8,128)(2,1)S(1)}, u32[]{:S(2)}, u32[]{:S(2)}) collective-permute-start(bf16[4,2,128,128]{3,2,1,0:T(8,128)(2,1)} %get-tuple-element.56), channel_id=1, source_target_pairs={{0,1},{1,0},{2,3},{3,2},{4,5},{5,4},{6,7},{7,6},{8,9},{9,8},{10,11... | collective-permute-start | bytes 786440 | tf_op jit(solution)/shard_map/ppermute | solution.py:301
  175.8 8.4 %collective-permute-start.23 = (bf16[4,2,128,128]{3,2,1,0:T(8,128)(2,1)}, bf16[4,2,128,128]{3,2,1,0:T(8,128)(2,1)S(1)}, u32[]{:S(2)}, u32[]{:S(2)}) collective-permute-start(bf16[4,2,128,128]{3,2,1,0:T(8,128)(2,1)} %get-tuple-element.49), channel_id=1, source_target_pairs={{0,1},{1,0},{2,3},{3,2},{4,5},{5,4},{6,7},{7,6},{8,9},{9,8},{10,11... | collective-permute-start | bytes 786440 | tf_op jit(solution)/shard_map/ppermute | solution.py:301
  176.9 9.9 %collective-permute-start.46 = (bf16[2,128,128]{2,1,0:T(8,128)(2,1)S(1)}, bf16[2,128,128]{2,1,0:T(8,128)(2,1)S(1)}, u32[]{:S(2)}, u32[]{:S(2)}) collective-permute-start(bf16[2,128,128]{2,1,0:T(8,128)(2,1)S(1)} %get-tuple-element.74), channel_id=1, source_target_pairs={{0,2},{1,3},{2,0},{3,1},{4,6},{5,7},{6,4},{7,5},{8,10},{9,11},{10,... | collective-permute-start | bytes 196616 | tf_op jit(solution)/shard_map/ppermute | solution.py:301
  178.4 9.0 %collective-permute-start.47 = (bf16[2,128,128]{2,1,0:T(8,128)(2,1)S(1)}, bf16[2,128,128]{2,1,0:T(8,128)(2,1)S(1)}, u32[]{:S(2)}, u32[]{:S(2)}) collective-permute-start(bf16[2,128,128]{2,1,0:T(8,128)(2,1)S(1)} %get-tuple-element.75), channel_id=1, source_target_pairs={{0,4},{1,5},{2,6},{3,7},{4,0},{5,1},{6,2},{7,3},{8,12},{9,13},{10,... | collective-permute-start | bytes 196616 | tf_op jit(solution)/shard_map/ppermute | solution.py:301
  179.9 8.9 %collective-permute-start.48 = (bf16[2,128,128]{2,1,0:T(8,128)(2,1)S(1)}, bf16[2,128,128]{2,1,0:T(8,128)(2,1)S(1)}, u32[]{:S(2)}, u32[]{:S(2)}) collective-permute-start(bf16[2,128,128]{2,1,0:T(8,128)(2,1)S(1)} %get-tuple-element.76), channel_id=1, source_target_pairs={{0,6},{1,7},{2,4},{3,5},{4,2},{5,3},{6,0},{7,1},{8,14},{9,15},{10,... | collective-permute-start | bytes 196616 | tf_op jit(solution)/shard_map/ppermute | solution.py:301
  181.5 8.9 %collective-permute-start.38 = (bf16[2,128,128]{2,1,0:T(8,128)(2,1)S(1)}, bf16[2,128,128]{2,1,0:T(8,128)(2,1)S(1)}, u32[]{:S(2)}, u32[]{:S(2)}) collective-permute-start(bf16[2,128,128]{2,1,0:T(8,128)(2,1)S(1)} %get-tuple-element.66), channel_id=1, source_target_pairs={{0,2},{1,3},{2,0},{3,1},{4,6},{5,7},{6,4},{7,5},{8,10},{9,11},{10,... | collective-permute-start | bytes 196616 | tf_op jit(solution)/shard_map/ppermute | solution.py:301
  184.2 6.8 %collective-permute-start.39 = (bf16[2,128,128]{2,1,0:T(8,128)(2,1)S(1)}, bf16[2,128,128]{2,1,0:T(8,128)(2,1)S(1)}, u32[]{:S(2)}, u32[]{:S(2)}) collective-permute-start(bf16[2,128,128]{2,1,0:T(8,128)(2,1)S(1)} %get-tuple-element.67), channel_id=1, source_target_pairs={{0,4},{1,5},{2,6},{3,7},{4,0},{5,1},{6,2},{7,3},{8,12},{9,13},{10,... | collective-permute-start | bytes 196616 | tf_op jit(solution)/shard_map/ppermute | solution.py:301
  186.8 5.7 %collective-permute-start.40 = (bf16[2,128,128]{2,1,0:T(8,128)(2,1)S(1)}, bf16[2,128,128]{2,1,0:T(8,128)(2,1)S(1)}, u32[]{:S(2)}, u32[]{:S(2)}) collective-permute-start(bf16[2,128,128]{2,1,0:T(8,128)(2,1)S(1)} %get-tuple-element.68), channel_id=1, source_target_pairs={{0,6},{1,7},{2,4},{3,5},{4,2},{5,3},{6,0},{7,1},{8,14},{9,15},{10,... | collective-permute-start | bytes 196616 | tf_op jit(solution)/shard_map/ppermute | solution.py:301
  187.4 6.7 %collective-permute-start.31 = (bf16[2,128,128]{2,1,0:T(8,128)(2,1)S(1)}, bf16[2,128,128]{2,1,0:T(8,128)(2,1)S(1)}, u32[]{:S(2)}, u32[]{:S(2)}) collective-permute-start(bf16[2,128,128]{2,1,0:T(8,128)(2,1)S(1)} %get-tuple-element.58), channel_id=1, source_target_pairs={{0,2},{1,3},{2,0},{3,1},{4,6},{5,7},{6,4},{7,5},{8,10},{9,11},{10,... | collective-permute-start | bytes 196616 | tf_op jit(solution)/shard_map/ppermute | solution.py:301
  188.9 5.7 %collective-permute-start.32 = (bf16[2,128,128]{2,1,0:T(8,128)(2,1)S(1)}, bf16[2,128,128]{2,1,0:T(8,128)(2,1)S(1)}, u32[]{:S(2)}, u32[]{:S(2)}) collective-permute-start(bf16[2,128,128]{2,1,0:T(8,128)(2,1)S(1)} %get-tuple-element.59), channel_id=1, source_target_pairs={{0,4},{1,5},{2,6},{3,7},{4,0},{5,1},{6,2},{7,3},{8,12},{9,13},{10,... | collective-permute-start | bytes 196616 | tf_op jit(solution)/shard_map/ppermute | solution.py:301
  190.4 5.9 %collective-permute-start.33 = (bf16[2,128,128]{2,1,0:T(8,128)(2,1)S(1)}, bf16[2,128,128]{2,1,0:T(8,128)(2,1)S(1)}, u32[]{:S(2)}, u32[]{:S(2)}) collective-permute-start(bf16[2,128,128]{2,1,0:T(8,128)(2,1)S(1)} %get-tuple-element.60), channel_id=1, source_target_pairs={{0,6},{1,7},{2,4},{3,5},{4,2},{5,3},{6,0},{7,1},{8,14},{9,15},{10,... | collective-permute-start | bytes 196616 | tf_op jit(solution)/shard_map/ppermute | solution.py:301
  191.0 5.4 %collective-permute-start.24 = (bf16[2,128,128]{2,1,0:T(8,128)(2,1)S(1)}, bf16[2,128,128]{2,1,0:T(8,128)(2,1)S(1)}, u32[]{:S(2)}, u32[]{:S(2)}) collective-permute-start(bf16[2,128,128]{2,1,0:T(8,128)(2,1)S(1)} %get-tuple-element.51), channel_id=1, source_target_pairs={{0,2},{1,3},{2,0},{3,1},{4,6},{5,7},{6,4},{7,5},{8,10},{9,11},{10,... | collective-permute-start | bytes 196616 | tf_op jit(solution)/shard_map/ppermute | solution.py:301
  192.5 4.6 %collective-permute-start.25 = (bf16[2,128,128]{2,1,0:T(8,128)(2,1)S(1)}, bf16[2,128,128]{2,1,0:T(8,128)(2,1)S(1)}, u32[]{:S(2)}, u32[]{:S(2)}) collective-permute-start(bf16[2,128,128]{2,1,0:T(8,128)(2,1)S(1)} %get-tuple-element.52), channel_id=1, source_target_pairs={{0,4},{1,5},{2,6},{3,7},{4,0},{5,1},{6,2},{7,3},{8,12},{9,13},{10,... | collective-permute-start | bytes 196616 | tf_op jit(solution)/shard_map/ppermute | solution.py:301
  194.1 5.2 %collective-permute-start.26 = (bf16[2,128,128]{2,1,0:T(8,128)(2,1)S(1)}, bf16[2,128,128]{2,1,0:T(8,128)(2,1)S(1)}, u32[]{:S(2)}, u32[]{:S(2)}) collective-permute-start(bf16[2,128,128]{2,1,0:T(8,128)(2,1)S(1)} %get-tuple-element.53), channel_id=1, source_target_pairs={{0,6},{1,7},{2,4},{3,5},{4,2},{5,3},{6,0},{7,1},{8,14},{9,15},{10,... | collective-permute-start | bytes 196616 | tf_op jit(solution)/shard_map/ppermute | solution.py:301
  194.6 6.1 %collective-permute-start.49 = (bf16[1,128,128]{2,1,0:T(8,128)(2,1)S(1)}, bf16[1,128,128]{2,1,0:T(8,128)(2,1)S(1)}, u32[]{:S(2)}, u32[]{:S(2)}) collective-permute-start(bf16[1,128,128]{2,1,0:T(8,128)(2,1)S(1)} %slice.174), channel_id=1, source_target_pairs={{0,8},{24,16},{1,9},{25,17},{2,10},{26,18},{3,11},{27,19},{4,12},{... | collective-permute-start | bytes 98312 | tf_op jit(solution)/shard_map/ppermute | solution.py:374
  199.4 3.5 %collective-permute-start.41 = (bf16[3,128,128]{2,1,0:T(8,128)(2,1)S(1)}, bf16[3,128,128]{2,1,0:T(8,128)(2,1)S(1)}, u32[]{:S(2)}, u32[]{:S(2)}) collective-permute-start(bf16[3,128,128]{2,1,0:T(8,128)(2,1)S(1)} %pad_maximum_fusion.3), channel_id=1, source_target_pairs={{0,8},{24,16},{1,9},{25,17},{2,10},{26,18},{3,11},{27,19},{4,12},{... | collective-permute-start | bytes 294920 | tf_op jit(solution)/shard_map/ppermute | solution.py:374
  (9 other events, 9.1 us)

commit v2 on v1

v2 whole, which is shorter than its diff:
```python
import math

import jax
import jax.numpy as jnp
import numpy as np
from jax import lax
from jax.experimental import pallas as pl
from jax.experimental.pallas import tpu as pltpu
from jax.sharding import PartitionSpec as P


HEAD = 128
QBLK = 32
PARTS = 2
CLIP = 2.5
EPS = 1e-06


f32 = jnp.float32
bf16 = jnp.bfloat16
HI = lax.Precision.HIGHEST
BIG = pltpu.CompilerParams(vmem_limit_bytes=60 * 1024 * 1024)


def signs(length):
    idx = np.arange(length)
    common = idx[:, None] & idx[None, :]
    parity = np.zeros((length, length), np.int64)
    for pos in range(length.bit_length() - 1):
        parity += (common >> pos) & 1
    return (1 - 2 * (parity % 2)).astype(np.float32)


def block_mean_matrix(rows):
    lane = np.arange(128)
    return ((lane[:, None] // QBLK) == (lane[None, :] // QBLK)).astype(np.float32) / (QBLK * rows)


def three_parts(x):
    high = x.astype(bf16)
    rest = x - high.astype(f32)
    middle = rest.astype(bf16)
    low = (rest - middle.astype(f32)).astype(bf16)
    return jnp.concatenate([high, middle, low], axis=0)


def clipped_tiles(value, mean_matrix):
    heads = value.shape[0] // HEAD
    groups = value.shape[1] // 128
    tiles = [
        value[h * HEAD : (h + 1) * HEAD, g * 128 : (g + 1) * 128] for h in range(heads) for g in range(groups)
    ]
    rows = [jnp.sum(x * x, axis=0, keepdims=True) for x in tiles]
    pad = -len(rows) % 8
    if pad:
        rows.append(jnp.zeros((pad, 128), f32))
    squares = jnp.concatenate(rows, axis=0)
    count = squares.shape[0]
    parts = jnp.dot(three_parts(squares), mean_matrix, preferred_element_type=f32)
    means = parts[:count] + parts[count : 2 * count] + parts[2 * count :]
    bounds = CLIP * jnp.sqrt(means + EPS)
    for at, x in enumerate(tiles):
        limit = bounds[at : at + 1]
        yield at // groups, at % groups, jnp.minimum(jnp.maximum(x, -limit), limit).astype(bf16)


def scale_kernel(scales_ref, codes_ref, out_ref):
    blocks = codes_ref.shape[0] // QBLK
    heads = codes_ref.shape[1] // HEAD
    for b in range(blocks):
        for h in range(heads):
            tile = codes_ref[b * QBLK : (b + 1) * QBLK, h * HEAD : (h + 1) * HEAD].astype(f32)
            out_ref[b * QBLK : (b + 1) * QBLK, h * HEAD : (h + 1) * HEAD] = (tile * scales_ref[b, h]).astype(bf16)


def scaled(codes, scales):
    return pl.pallas_call(
        scale_kernel,
        out_shape=jax.ShapeDtypeStruct(codes.shape, bf16),
        in_specs=[pl.BlockSpec(memory_space=pltpu.SMEM), pl.BlockSpec(memory_space=pltpu.VMEM)],
        out_specs=pl.BlockSpec(memory_space=pltpu.VMEM),
        name="scale_rows",
    )(scales, codes)


def piece_copies(n, m, r, x, where_ref, tok_hbm, parts, tv, wv, sem):
    gi, pair, parity = where_ref[0], where_ref[1] // 2, lax.rem(where_ref[1], 2)
    copies = []
    size = r // PARTS

    def add(source, target):
        copies.append(pltpu.make_async_copy(source, target, sem.at[len(copies)]))

    for a in range(n):
        col = (lax.rem(gi - a + n, n) * (m // 2) + jnp.bitwise_xor(pair, x)) * (2 * r)
        for p in range(PARTS):
            for flipped in range(2):
                row = 2 * a * r + jnp.where(parity == flipped, 0, r) + p * size
                add(parts[2 * p + flipped].at[a], wv.at[pl.ds(pl.multiple_of(row, 16), size)])
        add(tok_hbm.at[:, pl.ds(pl.multiple_of(col, 128), 2 * r)], tv.at[:, pl.ds(a * 2 * r, 2 * r)])
    for c in copies:
        c.start()
    return copies


def gather_dot_kernel(n, m, r, where_ref, tok_hbm, *refs):
    parts = refs[: 2 * PARTS]
    acc_ref, w_ref, tv, sem = refs[2 * PARTS :]
    for c in piece_copies(n, m, r, 0, where_ref, tok_hbm, parts, tv, w_ref, sem):
        c.wait()
    acc_ref[...] = jnp.dot(tv[...], w_ref[...], preferred_element_type=f32)


def gather_dot(n, m, r, where, tokens, parts):
    tok = tokens.shape[0]
    kv = parts[0].shape[-1]
    vm = pl.BlockSpec(memory_space=pltpu.VMEM)
    hbm = pl.BlockSpec(memory_space=pltpu.HBM)
    rows = n * 2 * r
    return pl.pallas_call(
        lambda *a: gather_dot_kernel(n, m, r, *a),
        out_shape=(jax.ShapeDtypeStruct((tok, kv), f32), jax.ShapeDtypeStruct((rows, kv), bf16)),
        in_specs=[pl.BlockSpec(memory_space=pltpu.SMEM), hbm] + [hbm] * len(parts),
        out_specs=(vm, vm),
        scratch_shapes=[pltpu.VMEM((tok, rows), bf16), pltpu.SemaphoreType.DMA((n * (2 * PARTS + 1),))],
        compiler_params=BIG,
        name="gather_dot",
    )(where, tokens, *parts)


def norm_kernel(n, m, r, xs, where_ref, tok_hbm, gain_ref, cot_ref, had_ref, mean_ref, acc_ref, *refs):
    heads = cot_ref.shape[1] // HEAD
    count = len(xs)
    parts, refs = refs[: 2 * PARTS * count], refs[2 * PARTS * count :]
    keys_ref, kg_ref, qt_ref = refs[:3]
    term_refs, refs = refs[3 : 3 + heads], refs[3 + heads :]
    w_refs, refs = refs[:count], refs[count:]
    fv, fsem, refs = refs[0], refs[1], refs[2:]
    side = where_ref[2]
    width = m * r
    nd = n // 2
    start = pl.multiple_of(jnp.where(side == 0, 0, n - nd) * width, 128)
    batches = []
    for p, x in enumerate(xs):
        mine = parts[2 * PARTS * p : 2 * PARTS * (p + 1)]
        batches.append(
            piece_copies(n, m, r, x, where_ref, tok_hbm, mine, refs[2 + p], w_refs[p], refs[0].at[p])
        )
    half = pltpu.make_async_copy(tok_hbm.at[:, pl.ds(start, nd * width)], fv, fsem)
    half.start()
    acc = refs[1] if count else acc_ref
    for p, batch in enumerate(batches):
        for c in batch:
            c.wait()
        base = acc if p else acc_ref
        acc[...] = base[...] + jnp.dot(refs[2 + p][...], w_refs[p][...], preferred_element_type=f32)
    gain = gain_ref[...]
    for h in range(heads):
        lanes = slice(h * HEAD, (h + 1) * HEAD)
        raw = acc[:, lanes]
        inv = lax.rsqrt(jnp.mean(raw * raw, axis=-1, keepdims=True) + EPS)
        unit = raw * inv
        keys_ref[:, lanes] = (unit * gain).astype(bf16)
        g = cot_ref[:, lanes].astype(f32) * gain
        kg = (inv * (g - unit * jnp.mean(g * unit, axis=-1, keepdims=True))).astype(bf16)
        kg_ref[:, lanes] = kg
        turned = lax.dot_general(had_ref[...], kg, (((1,), (1,)), ((), ())), preferred_element_type=f32)
        qt_ref[lanes, :] = (turned * (1.0 / math.sqrt(HEAD))).astype(bf16)
    half.wait()
    bw = min(width, 512)
    for d in range(nd):
        row = jnp.where(side == 0, d, nd - 1 - d)
        for b in range(width // bw):
            off = pl.multiple_of(row * width + b * bw, bw)
            value = jnp.dot(qt_ref[...], fv[:, pl.ds(off, bw)], preferred_element_type=f32)
            for h, g, y in clipped_tiles(value, mean_ref[...]):
                term_refs[h][d, :, b * bw + g * 128 : b * bw + (g + 1) * 128] = y


def norm_call(n, m, r, xs, where, tokens, gain, cot, had, mean, acc, parts):
    tok = tokens.shape[0]
    kv = acc.shape[1]
    heads = kv // HEAD
    nd = n // 2
    rows = n * 2 * r
    count = len(xs)
    vm = pl.BlockSpec(memory_space=pltpu.VMEM)
    hbm = pl.BlockSpec(memory_space=pltpu.HBM)
    shapes = [
        jax.ShapeDtypeStruct((tok, kv), bf16),
        jax.ShapeDtypeStruct((tok, kv), bf16),
        jax.ShapeDtypeStruct((kv, tok), bf16),
    ]
    shapes += [jax.ShapeDtypeStruct((nd, HEAD, m * r), bf16)] * heads
    shapes += [jax.ShapeDtypeStruct((rows, kv), bf16)] * count
    scratch = [pltpu.VMEM((tok, nd * m * r), bf16), pltpu.SemaphoreType.DMA]
    if count:
        scratch += [pltpu.SemaphoreType.DMA((count, n * (2 * PARTS + 1))), pltpu.VMEM((tok, kv), f32)]
        scratch += [pltpu.VMEM((tok, rows), bf16)] * count
    return pl.pallas_call(
        lambda *a: norm_kernel(n, m, r, xs, *a),
        out_shape=shapes,
        in_specs=[pl.BlockSpec(memory_space=pltpu.SMEM), hbm] + [vm] * 5 + [hbm] * len(parts),
        out_specs=[vm] * len(shapes),
        scratch_shapes=scratch,
        compiler_params=BIG,
        name="norm",
    )(where, tokens, gain, cot, had, mean, acc, *parts)


def term_kernel(groups, where_ref, tok_ref, *refs):
    mean_ref, out_refs = refs[groups], refs[groups + 1 :]
    at = 0
    for qt_ref in refs[:groups]:
        value = jnp.dot(qt_ref[...], tok_ref[...], preferred_element_type=f32)
        for h, g, x in clipped_tiles(value, mean_ref[...]):
            out_refs[at + h][0, :, g * 128 : (g + 1) * 128] = x
        at += qt_ref.shape[0] // HEAD


def term_call(n, m, r, where, tokens, qts, mean):
    tok = tokens.shape[0]
    rows = [q.shape[0] for q in qts]
    heads = sum(rows) // HEAD
    nd = n // 2
    width = m * r
    bw = min(1024, width)
    nb = width // bw

    def tok_index(d, b, where_ref):
        row = jnp.where(where_ref[2] == 0, n - 1 - d, d)
        return (0, row * nb + b)

    return pl.pallas_call(
        lambda *a: term_kernel(len(qts), *a),
        grid_spec=pltpu.PrefetchScalarGridSpec(
            num_scalar_prefetch=1,
            grid=(nd, nb),
            in_specs=[pl.BlockSpec((tok, bw), tok_index)]
            + [pl.BlockSpec((size, tok), lambda d, b, w: (0, 0)) for size in rows]
            + [pl.BlockSpec((128, 128), lambda d, b, w: (0, 0))],
            out_specs=[pl.BlockSpec((1, HEAD, bw), lambda d, b, w: (d, 0, b))] * heads,
        ),
        out_shape=[jax.ShapeDtypeStruct((nd, HEAD, width), bf16)] * heads,
        compiler_params=BIG,
        name="terms",
    )(where, tokens, *qts, mean)


def tgrad_kernel(n, m, r, xs, where_ref, kg_ref, *refs):
    out_hbm, slabs, sem = refs[-3:]
    gi, pair = where_ref[0], where_ref[1] // 2
    copies = []
    for p, x in enumerate(xs):
        for a in range(n):
            at = p * n + a
            col = (lax.rem(gi - a + n, n) * (m // 2) + jnp.bitwise_xor(pair, x)) * (2 * r)
            slabs[at] = lax.dot_general(
                kg_ref[...], refs[p][a * 2 * r : (a + 1) * 2 * r], (((1,), (1,)), ((), ())),
                preferred_element_type=f32,
            ).astype(bf16)
            copy = pltpu.make_async_copy(
                slabs.at[at], out_hbm.at[:, pl.ds(pl.multiple_of(col, 128), 2 * r)], sem.at[at]
            )
            copy.start()
            copies.append(copy)
    for c in copies:
        c.wait()


def tgrad_call(n, m, r, xs, where, kg, weights, filled, d_model):
    tok = kg.shape[0]
    vm = pl.BlockSpec(memory_space=pltpu.VMEM)
    hbm = pl.BlockSpec(memory_space=pltpu.HBM)
    extra = [] if filled is None else [filled]
    count = n * len(xs)
    return pl.pallas_call(
        lambda *a: tgrad_kernel(n, m, r, xs, *a),
        in_specs=[pl.BlockSpec(memory_space=pltpu.SMEM)] + [vm] * (1 + len(xs)) + [hbm] * len(extra),
        out_specs=hbm,
        out_shape=jax.ShapeDtypeStruct((tok, d_model), bf16),
        scratch_shapes=[pltpu.VMEM((count, tok, 2 * r), bf16), pltpu.SemaphoreType.DMA((count,))],
        input_output_aliases={2 + len(xs): 0} if extra else {},
        compiler_params=BIG,
        name="token_grad",
    )(where, kg, *weights, *extra)


def recode_kernel(aligned, n, where_ref, a_ref, b_ref, mean_ref, keep_ref, send_ref):
    pair, parity = where_ref[1] // 2, lax.rem(where_ref[1], 2)

    @pl.when(jnp.logical_or(where_ref[0] == 0, where_ref[0] == n - 1))
    def _():
        for d in range(a_ref.shape[0]):
            value = a_ref[d].astype(f32) + b_ref[d].astype(f32)
            tiles = [x for _, _, x in clipped_tiles(value, mean_ref[...])]
            for g, x in enumerate(tiles):
                if not aligned:
                    keep_ref[d, :, g * 128 : (g + 1) * 128] = x
                elif g % 2 == 0:
                    at = jnp.bitwise_xor(pair, g // 2)
                    keep_ref[at, d] = jnp.where(parity == 0, x, tiles[g + 1])
                    send_ref[at, d] = jnp.where(parity == 0, tiles[g + 1], x)


def recode_call(n, m, r, where, arrived, mine, mean):
    aligned = r == 128
    vm = pl.BlockSpec(memory_space=pltpu.VMEM)
    nd = arrived.shape[0]
    shape = (m // 2, nd, HEAD, r) if aligned else arrived.shape
    keep, send = pl.pallas_call(
        lambda *a: recode_kernel(aligned, n, *a),
        out_shape=(jax.ShapeDtypeStruct(shape, bf16),) * 2,
        in_specs=[pl.BlockSpec(memory_space=pltpu.SMEM), vm, vm, vm],
        out_specs=(vm, vm),
        name="recode",
    )(where, arrived, mine, mean)
    if not aligned:
        pairs = jnp.bitwise_xor(where[1] // 2, jnp.arange(m // 2, dtype=jnp.int32))
        blocks = keep.reshape(nd, HEAD, m, r).transpose(2, 0, 1, 3)
        parity = where[1] % 2
        keep = jnp.take(blocks, pairs * 2 + parity, axis=0)
        send = jnp.take(blocks, pairs * 2 + 1 - parity, axis=0)
    return keep, send


def body(tokens, codes, scales, gain, cotangent):
    n = lax.axis_size("gx")
    m = lax.axis_size("gy")
    gi = lax.axis_index("gx")
    gj = lax.axis_index("gy")
    r = codes.shape[0]
    kv = codes.shape[1]
    heads = kv // HEAD
    nd = n // 2
    barrier = lax.optimization_barrier

    _, d_model = tokens.shape
    pm = signs(HEAD)
    had = jnp.asarray(pm, bf16)
    mean = jnp.asarray(block_mean_matrix(HEAD), bf16)
    side = jnp.where(gi < nd, 1, 0)
    where = jnp.stack([gi, gj, side]).astype(jnp.int32)
    aligned = 2 * r % 128 == 0 and m == 8

    flip = lambda x, mask: lax.ppermute(x, "gy", [(j, j ^ mask) for j in range(m)])
    own = scaled(codes, scales)
    size = r // PARTS
    pieces = [[] for _ in range(m // 2)]
    for p in range(PARTS):
        mine = own[p * size : (p + 1) * size]
        near = [mine]
        for s in range(1, n):
            near.append(lax.ppermute(mine, "gx", [(i, (i + s) % n) for i in range(n)]))
        near = jnp.stack(near)
        for x in range(m // 2):
            piece = near
            if x:
                piece = flip(near, 2 * x)
            pieces[x] += [piece, flip(piece, 1)]
    norm_args = (where, tokens, gain.reshape(1, HEAD), cotangent, had, mean)
    if aligned:
        acc, w0 = gather_dot(n, m, r, where, tokens, pieces[0])
        keys, key_grad, qt, *first, w1, w2, w3 = norm_call(
            n, m, r, (1, 2, 3), *norm_args, acc, pieces[1] + pieces[2] + pieces[3]
        )
        weights = [w0, w1, w2, w3]
    else:
        rows = [jnp.concatenate(piece[q::2], axis=1) for piece in pieces for q in range(2)]
        block = jnp.stack(rows)
        block = jnp.take(block, jnp.bitwise_xor(gj, jnp.arange(m, dtype=jnp.int32)), axis=0)
        block = jnp.take(block, (gi - jnp.arange(n, dtype=jnp.int32)) % n, axis=1)
        weight = block.transpose(1, 0, 2, 3).reshape(d_model, kv)
        acc = jnp.dot(tokens, weight, preferred_element_type=f32)
        keys, key_grad, qt, *first = norm_call(n, m, r, (), *norm_args, acc, [])

    hops = n - 1
    arrived = {}

    def hop(g, k, pay):
        arrived[g, k] = lax.ppermute(pay, "gx", [(g, g + 1), (n - 1 - g, n - 2 - g)])

    exchange = flip
    kept, met, totals = {}, {}, {}

    def phase_a(k):
        keep, send = recode_call(n, m, r, where, arrived[hops - 1, k], second[k], mean)
        kept[k] = keep
        met[k] = exchange(send, 1)

    def phase_b(group):
        sums = [kept[k].astype(f32) + met[k].astype(f32) for k in group]
        join = lambda x: jnp.concatenate([w[x] for w in sums])
        blocks = barrier(tuple([join(0)] + [join(x).astype(bf16) for x in range(1, m // 2)]))
        total = blocks[0]
        for x in range(1, m // 2):
            total = total + exchange(blocks[x], 2 * x).astype(f32)
        for at, k in enumerate(group):
            totals[k] = total[at * nd : (at + 1) * nd]

    second = term_call(n, m, r, where, tokens, [qt], mean)
    token_grad = None
    if aligned:
        for xs in ((0, 1), (2,), (3,)):
            token_grad = tgrad_call(
                n, m, r, xs, where, key_grad, [weights[x] for x in xs], token_grad, d_model
            )
    else:
        token_grad = lax.dot_general(
            key_grad, weight, (((1,), (1,)), ((), ())), preferred_element_type=f32
        ).astype(bf16)
    for k in range(heads):
        hop(0, k, first[k])
        for g in range(1, hops):
            hop(g, k, arrived[g - 1, k] + (first if g < nd else second)[k])
        phase_a(k)
    for group in (list(range(heads - 2)), [heads - 2], [heads - 1]):
        phase_b(group)

    rotation = jnp.asarray(pm / np.float32(math.sqrt(HEAD)), f32)
    at_end = jnp.logical_or(gi == 0, gi == n - 1)
    out = []
    for batch in (list(range(heads)),):
        result = None
        for d in range(nd):
            value = jnp.stack([totals[k][d] for k in batch])
            if d == 0:
                value = jnp.where(at_end, value, 0.0)
            else:
                value = lax.ppermute(value.astype(bf16), "gx", [(0, d), (n - 1, n - 1 - d)]).astype(f32)
            result = value if result is None else result + value
        turned = jnp.einsum("har,ab->rhb", result, rotation, precision=HI)
        out.append(turned.reshape(r, len(batch) * HEAD))
    return keys, token_grad, jnp.concatenate(out, axis=1)


def solution(mesh):
    in_specs = (
        P(("gx", "gy"), None),
        P(("gx", "gy"), None),
        P(("gx", "gy"), None),
        P(),
        P(("gx", "gy"), None),
    )
    out_specs = (P(("gx", "gy"), None), P(("gx", "gy"), None), P(("gx", "gy"), None))

    return jax.shard_map(body, mesh=mesh, in_specs=in_specs, out_specs=out_specs, check_vma=False)
```

time: 205 us -> 203 us (level)
  waiting for transfers between devices: 69.3 us -> 81.6 us
  starting transfers between devices: 57 us -> 49.2 us
  Pallas kernels: 56.7 us -> 49.7 us
  other arithmetic: 12.5 us -> 15 us
    ppermute x30 -> x27, waiting for transfers between devices: 5.15 us -> 14.9 us  [body(): lax.ppermute(x, 'gy', [(j, j ^ mask) for j in range(m)])]
    pallas_call x8 -> x6, Pallas kernels: 45.1 us -> 38.2 us  [the longest x1 14 us: norm_call(): pl.pallas_call(lambda *a: norm_kernel(n, m, r, xs, *a), out_shape=shapes,...]
    ppermute x12, waiting for transfers between devices: 49 us -> 54.9 us  [hop(): lax.ppermute(pay, 'gx', [(g, g + 1), (n - 1 - g, n - 2 - g)])]
    ppermute x30 -> x27, starting transfers between devices: 25.6 us -> 19.8 us  [body(): lax.ppermute(x, 'gy', [(j, j ^ mask) for j in range(m)])]
    ppermute x6, waiting for transfers between devices: 13.3 us -> 9.29 us  [body(): near.append(lax.ppermute(mine, 'gx', [(i, (i + s) % n) for i in range(n)]))]
    add x8, other arithmetic: 6.89 us -> 10 us  [body(): hop(g, k, arrived[g - 1, k] + (first if g < nd else second)[k])]
    unnamed x46 -> x37, local copies, waits for them, and re-layouts: 4.59 us -> 3.99 us
    another operation x6 -> x7, other arithmetic: 4.18 us -> 4.25 us
  transfers between devices with their start and end apart: 50 -> 46, of which waited for: 19 -> 17; matrix products, arithmetic and copies ran while one was open for 6% -> 7% of each run, Pallas kernels for 18% -> 17%
where the time goes in v2:
time: 203 us; the launch traced here: 202 us
  waiting for transfers between devices  81.6 us (40%)
  Pallas kernels  49.7 us (24%)
  starting transfers between devices  49.2 us (24%)
  other arithmetic  15 us (7%)
  local copies, waits for them, and re-layouts  5.02 us (2%)
    ppermute x12, waiting for transfers between devices, hop(): lax.ppermute(pay, 'gx', [(g, g + 1), (n - 1 - g, n - 2 - g)])  54.9 us
    ppermute x27, starting transfers between devices, body(): lax.ppermute(x, 'gy', [(j, j ^ mask) for j in range(m)])  19.8 us
    ppermute x12, starting transfers between devices, hop(): lax.ppermute(pay, 'gx', [(g, g + 1), (n - 1 - g, n - 2 - g)])  15.9 us
    ppermute x27, waiting for transfers between devices, body(): lax.ppermute(x, 'gy', [(j, j ^ mask) for j in range(m)])  14.9 us
    pallas_call x1, Pallas kernels, norm_call(): pl.pallas_call(lambda *a: norm_kernel(n, m, r, xs, *a), out_shape=shapes,...  14 us
    pallas_call x3, Pallas kernels, tgrad_call(): pl.pallas_call(lambda *a: tgrad_kernel(n, m, r, xs, *a), in_specs=[pl.Blo...  12.4 us
    ppermute x6, starting transfers between devices, body(): near.append(lax.ppermute(mine, 'gx', [(i, (i + s) % n) for i in range(n)]))  12.1 us
    add x8, other arithmetic, body(): hop(g, k, arrived[g - 1, k] + (first if g < nd else second)[k])  10 us
  transfers between devices with their start and end apart: 46, of which 17 were waited for; matrix products, arithmetic and copies ran while one was open for 7% of the time, Pallas kernels for 17%

profile of v2, /device:TPU:0, one launch (start us, length us, event | category | flops | bytes accessed | tf_op | source)
XLA Modules:
  0.0 202.2 jit_solution(740740049393001165)
XLA Ops:
  0.6 1.6 scale_rows.1
  2.2 0.9 slice_bitcast_fusion.16
  3.1 4.1 %collective-permute-start.1 = (bf16[64,512]{1,0:T(8,128)(2,1)S(1)}, bf16[64,512]{1,0:T(8,128)(2,1)S(1)}, u32[]{:S(2)}, u32[]{:S(2)}) collective-permute-start(bf16[64,512]{1,0:T(8,128)(2,1)S(1)} %get-tuple-element.107), channel_id=1, source_target_pairs={{0,16},{8,24},{16,0},{24,8},{1,17},{9,25},{17,1},{25,9},{2,18},{10... | collective-permute-start | bytes 196616 | tf_op jit(solution)/shard_map/ppermute | solution.py:354
  7.3 1.6 collective-permute-start
  8.8 2.2 %collective-permute-start.2 = (bf16[64,512]{1,0:T(8,128)(2,1)S(1)}, bf16[64,512]{1,0:T(8,128)(2,1)S(1)}, u32[]{:S(2)}, u32[]{:S(2)}) collective-permute-start(bf16[64,512]{1,0:T(8,128)(2,1)S(1)} %get-tuple-element.107), channel_id=1, source_target_pairs={{0,24},{8,0},{16,8},{24,16},{1,25},{9,1},{17,9},{25,17},{2,26},{10... | collective-permute-start | bytes 196616 | tf_op jit(solution)/shard_map/ppermute | solution.py:354
  11.1 2.9 %collective-permute-done = bf16[64,512]{1,0:T(8,128)(2,1)S(1)} collective-permute-done((bf16[64,512]{1,0:T(8,128)(2,1)S(1)}, bf16[64,512]{1,0:T(8,128)(2,1)S(1)}, u32[]{:S(2)}, u32[]{:S(2)}) %collective-permute-start) | collective-permute-done | bytes 65568 | tf_op jit(solution)/shard_map/ppermute | solution.py:354
  14.0 2.5 %collective-permute-start.16 = (bf16[4,64,512]{2,1,0:T(8,128)(2,1)S(1)}, bf16[4,64,512]{2,1,0:T(8,128)(2,1)S(1)}, u32[]{:S(2)}, u32[]{:S(2)}) collective-permute-start(bf16[4,64,512]{2,1,0:T(8,128)(2,1)S(1)} %pad_maximum_fusion.a_2_), channel_id=1, source_target_pairs={{0,6},{1,7},{2,4},{3,5},{4,2},{5,3},{6,0},{7,1},{8,14},{9,15},{10,... | collective-permute-start | bytes 786440 | tf_op jit(solution)/shard_map/ppermute | solution.py:346
  17.6 2.2 %collective-permute-start.4 = (bf16[64,512]{1,0:T(8,128)(2,1)S(1)}, bf16[64,512]{1,0:T(8,128)(2,1)S(1)}, u32[]{:S(2)}, u32[]{:S(2)}) collective-permute-start(bf16[64,512]{1,0:T(8,128)(2,1)S(1)} %get-tuple-element.106), channel_id=1, source_target_pairs={{0,8},{8,16},{16,24},{24,0},{1,9},{9,17},{17,25},{25,1},{2,10},{10... | collective-permute-start | bytes 196616 | tf_op jit(solution)/shard_map/ppermute | solution.py:354
  19.7 4.1 %collective-permute-done.4 = bf16[64,512]{1,0:T(8,128)(2,1)S(1)} collective-permute-done((bf16[64,512]{1,0:T(8,128)(2,1)S(1)}, bf16[64,512]{1,0:T(8,128)(2,1)S(1)}, u32[]{:S(2)}, u32[]{:S(2)}) %collective-permute-start.4) | collective-permute-done | bytes 65568 | tf_op jit(solution)/shard_map/ppermute | solution.py:354
  23.9 2.0 collective-permute-start.6
  25.9 2.3 %collective-permute-done.6 = bf16[64,512]{1,0:T(8,128)(2,1)S(1)} collective-permute-done((bf16[64,512]{1,0:T(8,128)(2,1)S(1)}, bf16[64,512]{1,0:T(8,128)(2,1)S(1)}, u32[]{:S(2)}, u32[]{:S(2)}) %collective-permute-start.6) | collective-permute-done | bytes 65568 | tf_op jit(solution)/shard_map/ppermute | solution.py:354
  28.2 2.5 %collective-permute-start.18 = (bf16[4,64,512]{2,1,0:T(8,128)(2,1)S(1)}, bf16[4,64,512]{2,1,0:T(8,128)(2,1)S(1)}, u32[]{:S(2)}, u32[]{:S(2)}) collective-permute-start(bf16[4,64,512]{2,1,0:T(8,128)(2,1)S(1)} %pad_maximum_fusion.1.a_4_), channel_id=1, source_target_pairs={{0,6},{1,7},{2,4},{3,5},{4,2},{5,3},{6,0},{7,1},{8,14},{9,15},{10,... | collective-permute-start | bytes 786440 | tf_op jit(solution)/shard_map/ppermute | solution.py:346
  32.3 6.1 %collective-permute-done.18.a_17_ = bf16[4,64,512]{2,1,0:T(8,128)(2,1)S(1)} collective-permute-done((bf16[4,64,512]{2,1,0:T(8,128)(2,1)S(1)}, bf16[4,64,512]{2,1,0:T(8,128)(2,1)S(1)}, u32[]{:S(2)}, u32[]{:S(2)}) %collective-permute-start.18) | collective-permute-done | bytes 262176 | tf_op jit(solution)/shard_map/ppermute | solution.py:346
  38.4 3.4 %collective-permute-done.14.a_13_ = bf16[4,64,512]{2,1,0:T(8,128)(2,1)S(1)} collective-permute-done((bf16[4,64,512]{2,1,0:T(8,128)(2,1)S(1)}, bf16[4,64,512]{2,1,0:T(8,128)(2,1)S(1)}, u32[]{:S(2)}, u32[]{:S(2)}) %collective-permute-start.14) | collective-permute-done | bytes 262176 | tf_op jit(solution)/shard_map/ppermute | solution.py:346
  43.4 5.0 %gather_dot.1 = (f32[896,512]{1,0:T(8,128)}, bf16[1024,512]{1,0:T(8,128)(2,1)}) custom-call(s32[3]{0:T(128)} %pad_add_fusion.a_0_, bf16[896,4096]{1,0:T(8,128)(2,1)} %a_1_.5, bf16[4,64,512]{2,1,0:T(8,128)(2,1)} %copy-done, bf16[4,64,512]{2,1,0:T(8,128)(2,1)} %copy-done.5, bf16[4,64,512]{2,1,0:T(8,128)(2,1)} %copy-done.1, bf16[4,64,512]{2,1,0:T(8,128)(2,1)} %copy-done.7), custom_call_target="tpu_custom_call" | custom-call | tf_op jit(solution)/shard_map/gather_dot/pallas_call | solution.py:120
  49.2 14.0 %norm.1 = (bf16[896,512]{1,0:T(8,128)(2,1)}, bf16[896,512]{1,0:T(8,128)(2,1)}, bf16[512,896]{1,0:T(8,128)(2,1)}, bf16[2,128,1024]{2,1,0:T(8,128)(2,1)}, bf16[2,1...) custom-call(s32[3]{0:T(128)} %pad_add_fusion.a_0_, ...), custom_call_target="tpu_custom_call" | custom-call | tf_op jit(solution)/shard_map/norm/pallas_call | solution.py:200
  63.3 3.0 %collective-permute-start.38 = (bf16[2,128,1024]{2,1,0:T(8,128)(2,1)}, bf16[2,128,1024]{2,1,0:T(8,128)(2,1)S(1)}, u32[]{:S(2)}, u32[]{:S(2)}) collective-permute-start(bf16[2,128,1024]{2,1,0:T(8,128)(2,1)} %get-tuple-element.67), channel_id=1, source_target_pairs={{0,8},{24,16},{1,9},{25,17},{2,10},{26,18},{3,11},{27,19},{4,12},{... | collective-permute-start | bytes 1572872 | tf_op jit(solution)/shard_map/ppermute | solution.py:381
  66.3 1.3 collective-permute-start.31
  67.6 1.3 collective-permute-start.24
  69.0 1.3 collective-permute-start.20
  70.3 8.6 %collective-permute-done.38 = bf16[2,128,1024]{2,1,0:T(8,128)(2,1)S(1)} collective-permute-done((bf16[2,128,1024]{2,1,0:T(8,128)(2,1)}, bf16[2,128,1024]{2,1,0:T(8,128)(2,1)S(1)}, u32[]{:S(2)}, u32[]{:S(2)}) %collective-permute-start.38) | collective-permute-done | bytes 524320 | tf_op jit(solution)/shard_map/ppermute | solution.py:381
  78.9 1.2 add.81
  80.8 9.3 %collective-permute-done.31 = bf16[2,128,1024]{2,1,0:T(8,128)(2,1)S(1)} collective-permute-done((bf16[2,128,1024]{2,1,0:T(8,128)(2,1)}, bf16[2,128,1024]{2,1,0:T(8,128)(2,1)S(1)}, u32[]{:S(2)}, u32[]{:S(2)}) %collective-permute-start.31) | collective-permute-done | bytes 524320 | tf_op jit(solution)/shard_map/ppermute | solution.py:381
  90.1 1.2 add.75
  92.1 9.3 %collective-permute-done.24 = bf16[2,128,1024]{2,1,0:T(8,128)(2,1)S(1)} collective-permute-done((bf16[2,128,1024]{2,1,0:T(8,128)(2,1)}, bf16[2,128,1024]{2,1,0:T(8,128)(2,1)S(1)}, u32[]{:S(2)}, u32[]{:S(2)}) %collective-permute-start.24) | collective-permute-done | bytes 524320 | tf_op jit(solution)/shard_map/ppermute | solution.py:381
  101.4 1.2 add.69
  102.6 1.5 collective-permute-start.25
  104.1 7.6 %collective-permute-done.20 = bf16[2,128,1024]{2,1,0:T(8,128)(2,1)S(1)} collective-permute-done((bf16[2,128,1024]{2,1,0:T(8,128)(2,1)}, bf16[2,128,1024]{2,1,0:T(8,128)(2,1)S(1)}, u32[]{:S(2)}, u32[]{:S(2)}) %collective-permute-start.20) | collective-permute-done | bytes 524320 | tf_op jit(solution)/shard_map/ppermute | solution.py:381
  111.7 1.2 add.66
  113.7 6.7 %terms.1 = (bf16[2,128,1024]{2,1,0:T(8,128)(2,1)}, bf16[2,128,1024]{2,1,0:T(8,128)(2,1)}, bf16[2,128,1024]{2,1,0:T(8,128)(2,1)}, bf16[2,128,1024]{2,1,0:T(8,128)(2,1)}) custom-call(s32[3]{0:T(128)} %pad_add_fusion.a_0_, bf16[896,4096]{1,0:T(8,128)(2,1)} %a_1_.5, bf16[512,896]{1,0:T(8,128)(2,1)} %get-tuple-element.47.a_2_, ...), custom_call_target="tpu_custom_call" | custom-call | tf_op jit(solution)/shard_map/terms/pallas_call | solution.py:234
  120.4 1.2 add.82
  121.6 1.3 collective-permute-start.40
  122.9 1.2 add.76
  124.2 1.5 collective-permute-start.33
  125.7 1.4 add.70
  127.1 1.3 collective-permute-start.26
  128.4 1.2 add.67
  129.6 1.3 collective-permute-start.22
  130.9 10.2 %collective-permute-done.40.a_1_ = bf16[2,128,1024]{2,1,0:T(8,128)(2,1)} collective-permute-done((bf16[2,128,1024]{2,1,0:T(8,128)(2,1)S(1)}, bf16[2,128,1024]{2,1,0:T(8,128)(2,1)}, u32[]{:S(2)}, u32[]{:S(2)}) %collective-permute-start.40) | collective-permute-done | bytes 524320 | tf_op jit(solution)/shard_map/ppermute | solution.py:381
  141.1 2.5 %recode.7 = (bf16[4,2,128,128]{3,2,1,0:T(8,128)(2,1)}, bf16[4,2,128,128]{3,2,1,0:T(8,128)(2,1)}) custom-call(s32[3]{0:T(128)} %pad_add_fusion.a_0_, bf16[2,128,1024]{2,1,0:T(8,128)(2,1)} %collective-permute-done.40.a_1_, bf16[2,128,1024]{2,1,0:T(8,128)(2,1)} %get-tuple-element.68.a_2_, bf16[128,128]{1,0:T(8,128)(2,1)} %constant.25.clone.a_5_.a_3_), custom_call_target="tpu_custom_call" | custom-call | tf_op jit(solution)/shard_map/recode/pallas_call | solution.py:311
  143.6 5.1 %token_grad.3.a_3_ = bf16[896,4096]{1,0:T(8,128)(2,1)} custom-call(s32[3]{0:T(128)} %pad_add_fusion.a_0_, bf16[896,512]{1,0:T(8,128)(2,1)} %get-tuple-element.41.a_1_, bf16[1024,512]{1,0:T(8,128)(2,1)} %get-tuple-element.44.a_2_, bf16[1024,512]{1,0:T(8,128)(2,1)} %get-tuple-element.45.a_3_), custom_call_target="tpu_custom_call" | custom-call | tf_op jit(solution)/shard_map/token_grad/pallas_call | solution.py:277
  148.7 3.7 %token_grad.4.a_3_ = bf16[896,4096]{1,0:T(8,128)(2,1)} custom-call(s32[3]{0:T(128)} %pad_add_fusion.a_0_, bf16[896,512]{1,0:T(8,128)(2,1)} %get-tuple-element.41.a_1_, bf16[1024,512]{1,0:T(8,128)(2,1)} %get-tuple-element.43.a_2_, bf16[896,4096]{1,0:T(8,128)(2,1)} %token_grad.3.a_3_), custom_call_target="tpu_custom_call", output_to_operand_aliasing={{}: (3, {})} | custom-call | tf_op jit(solution)/shard_map/token_grad/pallas_call | solution.py:277
  152.4 3.7 %token_grad.5 = bf16[896,4096]{1,0:T(8,128)(2,1)} custom-call(s32[3]{0:T(128)} %pad_add_fusion.a_0_, bf16[896,512]{1,0:T(8,128)(2,1)} %get-tuple-element.41.a_1_, bf16[1024,512]{1,0:T(8,128)(2,1)} %get-tuple-element.42.a_2_, bf16[896,4096]{1,0:T(8,128)(2,1)} %token_grad.4.a_3_), custom_call_target="tpu_custom_call", output_to_operand_aliasing={{}: (3, {})} | custom-call | tf_op jit(solution)/shard_map/token_grad/pallas_call | solution.py:277
  156.9 2.5 %recode.6 = (bf16[4,2,128,128]{3,2,1,0:T(8,128)(2,1)}, bf16[4,2,128,128]{3,2,1,0:T(8,128)(2,1)}) custom-call(s32[3]{0:T(128)} %pad_add_fusion.a_0_, bf16[2,128,1024]{2,1,0:T(8,128)(2,1)} %copy-done.4, bf16[2,128,1024]{2,1,0:T(8,128)(2,1)} %get-tuple-element.60.a_2_, bf16[128,128]{1,0:T(8,128)(2,1)} %constant.25.clone.a_5_.a_3_), custom_call_target="tpu_custom_call" | custom-call | tf_op jit(solution)/shard_map/recode/pallas_call | solution.py:311
  159.9 3.6 %collective-permute-done.26.a_1_ = bf16[2,128,1024]{2,1,0:T(8,128)(2,1)S(1)} collective-permute-done((bf16[2,128,1024]{2,1,0:T(8,128)(2,1)S(1)}, bf16[2,128,1024]{2,1,0:T(8,128)(2,1)S(1)}, u32[]{:S(2)}, u32[]{:S(2)}) %collective-permute-start.26) | collective-permute-done | bytes 524320 | tf_op jit(solution)/shard_map/ppermute | solution.py:381
  164.3 2.5 %recode.5 = (bf16[4,2,128,128]{3,2,1,0:T(8,128)(2,1)}, bf16[4,2,128,128]{3,2,1,0:T(8,128)(2,1)}) custom-call(s32[3]{0:T(128)} %pad_add_fusion.a_0_, bf16[2,128,1024]{2,1,0:T(8,128)(2,1)} %copy-done.3, bf16[2,128,1024]{2,1,0:T(8,128)(2,1)} %get-tuple-element.52.a_2_, bf16[128,128]{1,0:T(8,128)(2,1)} %constant.25.clone.a_5_.a_3_), custom_call_target="tpu_custom_call" | custom-call | tf_op jit(solution)/shard_map/recode/pallas_call | solution.py:311
  166.8 6.3 %collective-permute-done.22.a_1_ = bf16[2,128,1024]{2,1,0:T(8,128)(2,1)S(1)} collective-permute-done((bf16[2,128,1024]{2,1,0:T(8,128)(2,1)S(1)}, bf16[2,128,1024]{2,1,0:T(8,128)(2,1)S(1)}, u32[]{:S(2)}, u32[]{:S(2)}) %collective-permute-start.22) | collective-permute-done | bytes 524320 | tf_op jit(solution)/shard_map/ppermute | solution.py:381
  173.9 2.5 %recode.4 = (bf16[4,2,128,128]{3,2,1,0:T(8,128)(2,1)}, bf16[4,2,128,128]{3,2,1,0:T(8,128)(2,1)}) custom-call(s32[3]{0:T(128)} %pad_add_fusion.a_0_, bf16[2,128,1024]{2,1,0:T(8,128)(2,1)} %copy-done.2, bf16[2,128,1024]{2,1,0:T(8,128)(2,1)} %get-tuple-element.48.a_2_, bf16[128,128]{1,0:T(8,128)(2,1)} %constant.25.clone.a_5_.a_3_), custom_call_target="tpu_custom_call" | custom-call | tf_op jit(solution)/shard_map/recode/pallas_call | solution.py:311
  176.4 1.0 fusion.17
  177.5 1.5 collective-permute-start.42
  179.9 1.2 collective-permute-start.44
  181.1 1.0 fusion.16
  182.2 1.5 collective-permute-start.35
  183.7 1.0 fusion.15
  184.8 0.9 collective-permute-start.36
  185.6 1.0 fusion.14
  186.8 1.3 collective-permute-start.37
  188.1 1.5 collective-permute-start.28
  190.5 1.3 collective-permute-start.30
  191.7 1.1 collective-permute-done.37
  192.9 1.9 collective-permute-done.28
  194.9 2.2 %collective-permute-done.29 = bf16[4,128,128]{2,1,0:T(8,128)(2,1)S(1)} collective-permute-done((bf16[4,128,128]{2,1,0:T(8,128)(2,1)S(1)}, bf16[4,128,128]{2,1,0:T(8,128)(2,1)S(1)}, u32[]{:S(2)}, u32[]{:S(2)}) %collective-permute-start.29) | collective-permute-done | bytes 131104 | tf_op jit(solution)/shard_map/ppermute | solution.py:346
  197.2 1.3 collective-permute-start.45
  198.5 2.5 %collective-permute-done.45 = bf16[4,128,128]{2,1,0:T(8,128)(2,1)S(1)} collective-permute-done((bf16[4,128,128]{2,1,0:T(8,128)(2,1)S(1)}, bf16[4,128,128]{2,1,0:T(8,128)(2,1)S(1)}, u32[]{:S(2)}, u32[]{:S(2)}) %collective-permute-start.45) | collective-permute-done | bytes 131104 | tf_op jit(solution)/shard_map/ppermute | solution.py:430
  (113 shorter events, 13.3 us)
Async XLA Ops:
  3.1 8.0 %collective-permute-start.1 = (bf16[64,512]{1,0:T(8,128)(2,1)S(1)}, bf16[64,512]{1,0:T(8,128)(2,1)S(1)}, u32[]{:S(2)}, u32[]{:S(2)}) collective-permute-start(bf16[64,512]{1,0:T(8,128)(2,1)S(1)} %get-tuple-element.107), channel_id=1, source_target_pairs={{0,16},{8,24},{16,0},{24,8},{1,17},{9,25},{17,1},{25,9},{2,18},{10... | collective-permute-start | bytes 196616 | tf_op jit(solution)/shard_map/ppermute | solution.py:354
  7.3 6.7 %collective-permute-start = (bf16[64,512]{1,0:T(8,128)(2,1)S(1)}, bf16[64,512]{1,0:T(8,128)(2,1)S(1)}, u32[]{:S(2)}, u32[]{:S(2)}) collective-permute-start(bf16[64,512]{1,0:T(8,128)(2,1)S(1)} %get-tuple-element.107), channel_id=1, source_target_pairs={{0,8},{8,16},{16,24},{24,0},{1,9},{9,17},{17,25},{25,1},{2,10},{10... | collective-permute-start | bytes 196616 | tf_op jit(solution)/shard_map/ppermute | solution.py:354
  8.8 5.1 %collective-permute-start.2 = (bf16[64,512]{1,0:T(8,128)(2,1)S(1)}, bf16[64,512]{1,0:T(8,128)(2,1)S(1)}, u32[]{:S(2)}, u32[]{:S(2)}) collective-permute-start(bf16[64,512]{1,0:T(8,128)(2,1)S(1)} %get-tuple-element.107), channel_id=1, source_target_pairs={{0,24},{8,0},{16,8},{24,16},{1,25},{9,1},{17,9},{25,17},{2,26},{10... | collective-permute-start | bytes 196616 | tf_op jit(solution)/shard_map/ppermute | solution.py:354
  11.1 6.5 %collective-permute-start.5 = (bf16[64,512]{1,0:T(8,128)(2,1)S(1)}, bf16[64,512]{1,0:T(8,128)(2,1)S(1)}, u32[]{:S(2)}, u32[]{:S(2)}) collective-permute-start(bf16[64,512]{1,0:T(8,128)(2,1)S(1)} %get-tuple-element.106), channel_id=1, source_target_pairs={{0,16},{8,24},{16,0},{24,8},{1,17},{9,25},{17,1},{25,9},{2,18},{10... | collective-permute-start | bytes 196616 | tf_op jit(solution)/shard_map/ppermute | solution.py:354
  14.0 29.4 %copy-start = (bf16[4,64,512]{2,1,0:T(8,128)(2,1)}, bf16[4,64,512]{2,1,0:T(8,128)(2,1)S(1)}, u32[]{:S(2)}) copy-start(bf16[4,64,512]{2,1,0:T(8,128)(2,1)S(1)} %pad_maximum_fusion.a_2_) | copy-start | bytes 786436
  14.0 16.7 %collective-permute-start.16 = (bf16[4,64,512]{2,1,0:T(8,128)(2,1)S(1)}, bf16[4,64,512]{2,1,0:T(8,128)(2,1)S(1)}, u32[]{:S(2)}, u32[]{:S(2)}) collective-permute-start(bf16[4,64,512]{2,1,0:T(8,128)(2,1)S(1)} %pad_maximum_fusion.a_2_), channel_id=1, source_target_pairs={{0,6},{1,7},{2,4},{3,5},{4,2},{5,3},{6,0},{7,1},{8,14},{9,15},{10,... | collective-permute-start | bytes 786440 | tf_op jit(solution)/shard_map/ppermute | solution.py:346
  16.5 14.7 %collective-permute-start.12 = (bf16[4,64,512]{2,1,0:T(8,128)(2,1)S(1)}, bf16[4,64,512]{2,1,0:T(8,128)(2,1)S(1)}, u32[]{:S(2)}, u32[]{:S(2)}) collective-permute-start(bf16[4,64,512]{2,1,0:T(8,128)(2,1)S(1)} %pad_maximum_fusion.a_2_), channel_id=1, source_target_pairs={{0,4},{1,5},{2,6},{3,7},{4,0},{5,1},{6,2},{7,3},{8,12},{9,13},{10,... | collective-permute-start | bytes 786440 | tf_op jit(solution)/shard_map/ppermute | solution.py:346
  17.0 14.7 %collective-permute-start.8 = (bf16[4,64,512]{2,1,0:T(8,128)(2,1)S(1)}, bf16[4,64,512]{2,1,0:T(8,128)(2,1)S(1)}, u32[]{:S(2)}, u32[]{:S(2)}) collective-permute-start(bf16[4,64,512]{2,1,0:T(8,128)(2,1)S(1)} %pad_maximum_fusion.a_2_), channel_id=1, source_target_pairs={{0,2},{1,3},{2,0},{3,1},{4,6},{5,7},{6,4},{7,5},{8,10},{9,11},{10,... | collective-permute-start | bytes 786440 | tf_op jit(solution)/shard_map/ppermute | solution.py:346
  17.6 14.2 %collective-permute-start.3 = (bf16[4,64,512]{2,1,0:T(8,128)(2,1)S(1)}, bf16[4,64,512]{2,1,0:T(8,128)(2,1)S(1)}, u32[]{:S(2)}, u32[]{:S(2)}) collective-permute-start(bf16[4,64,512]{2,1,0:T(8,128)(2,1)S(1)} %pad_maximum_fusion.a_2_), channel_id=1, source_target_pairs={{0,1},{1,0},{2,3},{3,2},{4,5},{5,4},{6,7},{7,6},{8,9},{9,8},{10,11... | collective-permute-start | bytes 786440 | tf_op jit(solution)/shard_map/ppermute | solution.py:346
  17.6 6.3 %collective-permute-start.4 = (bf16[64,512]{1,0:T(8,128)(2,1)S(1)}, bf16[64,512]{1,0:T(8,128)(2,1)S(1)}, u32[]{:S(2)}, u32[]{:S(2)}) collective-permute-start(bf16[64,512]{1,0:T(8,128)(2,1)S(1)} %get-tuple-element.106), channel_id=1, source_target_pairs={{0,8},{8,16},{16,24},{24,0},{1,9},{9,17},{17,25},{25,1},{2,10},{10... | collective-permute-start | bytes 196616 | tf_op jit(solution)/shard_map/ppermute | solution.py:354
  23.9 4.3 %collective-permute-start.6 = (bf16[64,512]{1,0:T(8,128)(2,1)S(1)}, bf16[64,512]{1,0:T(8,128)(2,1)S(1)}, u32[]{:S(2)}, u32[]{:S(2)}) collective-permute-start(bf16[64,512]{1,0:T(8,128)(2,1)S(1)} %get-tuple-element.106), channel_id=1, source_target_pairs={{0,24},{8,0},{16,8},{24,16},{1,25},{9,1},{17,9},{25,17},{2,26},{10... | collective-permute-start | bytes 196616 | tf_op jit(solution)/shard_map/ppermute | solution.py:354
  28.2 15.2 %copy-start.1 = (bf16[4,64,512]{2,1,0:T(8,128)(2,1)}, bf16[4,64,512]{2,1,0:T(8,128)(2,1)S(1)}, u32[]{:S(2)}) copy-start(bf16[4,64,512]{2,1,0:T(8,128)(2,1)S(1)} %pad_maximum_fusion.1.a_4_) | copy-start | bytes 786436
  28.2 10.2 %collective-permute-start.18 = (bf16[4,64,512]{2,1,0:T(8,128)(2,1)S(1)}, bf16[4,64,512]{2,1,0:T(8,128)(2,1)S(1)}, u32[]{:S(2)}, u32[]{:S(2)}) collective-permute-start(bf16[4,64,512]{2,1,0:T(8,128)(2,1)S(1)} %pad_maximum_fusion.1.a_4_), channel_id=1, source_target_pairs={{0,6},{1,7},{2,4},{3,5},{4,2},{5,3},{6,0},{7,1},{8,14},{9,15},{10,... | collective-permute-start | bytes 786440 | tf_op jit(solution)/shard_map/ppermute | solution.py:346
  30.7 17.8 %copy-start.8 = (bf16[4,64,512]{2,1,0:T(8,128)(2,1)}, bf16[4,64,512]{2,1,0:T(8,128)(2,1)S(1)}, u32[]{:S(2)}) copy-start(bf16[4,64,512]{2,1,0:T(8,128)(2,1)S(1)} %collective-permute-done.16.a_15_) | copy-start | bytes 786436
  30.7 11.1 %collective-permute-start.14 = (bf16[4,64,512]{2,1,0:T(8,128)(2,1)S(1)}, bf16[4,64,512]{2,1,0:T(8,128)(2,1)S(1)}, u32[]{:S(2)}, u32[]{:S(2)}) collective-permute-start(bf16[4,64,512]{2,1,0:T(8,128)(2,1)S(1)} %pad_maximum_fusion.1.a_4_), channel_id=1, source_target_pairs={{0,4},{1,5},{2,6},{3,7},{4,0},{5,1},{6,2},{7,3},{8,12},{9,13},{10,... | collective-permute-start | bytes 786440 | tf_op jit(solution)/shard_map/ppermute | solution.py:346
  31.2 17.3 %copy-start.9 = (bf16[4,64,512]{2,1,0:T(8,128)(2,1)}, bf16[4,64,512]{2,1,0:T(8,128)(2,1)S(1)}, u32[]{:S(2)}) copy-start(bf16[4,64,512]{2,1,0:T(8,128)(2,1)S(1)} %collective-permute-done.12.a_11_) | copy-start | bytes 786436
  31.2 10.7 %collective-permute-start.10 = (bf16[4,64,512]{2,1,0:T(8,128)(2,1)S(1)}, bf16[4,64,512]{2,1,0:T(8,128)(2,1)S(1)}, u32[]{:S(2)}, u32[]{:S(2)}) collective-permute-start(bf16[4,64,512]{2,1,0:T(8,128)(2,1)S(1)} %pad_maximum_fusion.1.a_4_), channel_id=1, source_target_pairs={{0,2},{1,3},{2,0},{3,1},{4,6},{5,7},{6,4},{7,5},{8,10},{9,11},{10,... | collective-permute-start | bytes 786440 | tf_op jit(solution)/shard_map/ppermute | solution.py:346
  31.8 16.8 %copy-start.10 = (bf16[4,64,512]{2,1,0:T(8,128)(2,1)}, bf16[4,64,512]{2,1,0:T(8,128)(2,1)S(1)}, u32[]{:S(2)}) copy-start(bf16[4,64,512]{2,1,0:T(8,128)(2,1)S(1)} %collective-permute-done.8.a_7_) | copy-start | bytes 786436
  31.8 10.5 %collective-permute-start.7 = (bf16[4,64,512]{2,1,0:T(8,128)(2,1)S(1)}, bf16[4,64,512]{2,1,0:T(8,128)(2,1)S(1)}, u32[]{:S(2)}, u32[]{:S(2)}) collective-permute-start(bf16[4,64,512]{2,1,0:T(8,128)(2,1)S(1)} %pad_maximum_fusion.1.a_4_), channel_id=1, source_target_pairs={{0,1},{1,0},{2,3},{3,2},{4,5},{5,4},{6,7},{7,6},{8,9},{9,8},{10,11... | collective-permute-start | bytes 786440 | tf_op jit(solution)/shard_map/ppermute | solution.py:346
  31.8 11.6 %copy-start.5 = (bf16[4,64,512]{2,1,0:T(8,128)(2,1)}, bf16[4,64,512]{2,1,0:T(8,128)(2,1)S(1)}, u32[]{:S(2)}) copy-start(bf16[4,64,512]{2,1,0:T(8,128)(2,1)S(1)} %collective-permute-done.3.a_3_) | copy-start | bytes 786436
  31.8 10.6 %collective-permute-start.17 = (bf16[4,64,512]{2,1,0:T(8,128)(2,1)S(1)}, bf16[4,64,512]{2,1,0:T(8,128)(2,1)S(1)}, u32[]{:S(2)}, u32[]{:S(2)}) collective-permute-start(bf16[4,64,512]{2,1,0:T(8,128)(2,1)S(1)} %collective-permute-done.16.a_15_), channel_id=1, source_target_pairs={{0,1},{1,0},{2,3},{3,2},{4,5},{5,4},{6,7},{7,6},{8,9},{9,8},{10,11... | collective-permute-start | bytes 786440 | tf_op jit(solution)/shard_map/ppermute | solution.py:346
  38.4 10.2 %copy-start.11 = (bf16[4,64,512]{2,1,0:T(8,128)(2,1)}, bf16[4,64,512]{2,1,0:T(8,128)(2,1)S(1)}, u32[]{:S(2)}) copy-start(bf16[4,64,512]{2,1,0:T(8,128)(2,1)S(1)} %collective-permute-done.18.a_17_) | copy-start | bytes 786436
  38.4 10.1 %collective-permute-start.13 = (bf16[4,64,512]{2,1,0:T(8,128)(2,1)S(1)}, bf16[4,64,512]{2,1,0:T(8,128)(2,1)S(1)}, u32[]{:S(2)}, u32[]{:S(2)}) collective-permute-start(bf16[4,64,512]{2,1,0:T(8,128)(2,1)S(1)} %collective-permute-done.12.a_11_), channel_id=1, source_target_pairs={{0,1},{1,0},{2,3},{3,2},{4,5},{5,4},{6,7},{7,6},{8,9},{9,8},{10,11... | collective-permute-start | bytes 786440 | tf_op jit(solution)/shard_map/ppermute | solution.py:346
  41.8 6.8 %copy-start.12 = (bf16[4,64,512]{2,1,0:T(8,128)(2,1)}, bf16[4,64,512]{2,1,0:T(8,128)(2,1)S(1)}, u32[]{:S(2)}) copy-start(bf16[4,64,512]{2,1,0:T(8,128)(2,1)S(1)} %collective-permute-done.14.a_13_) | copy-start | bytes 786436
  41.8 6.7 %collective-permute-start.9 = (bf16[4,64,512]{2,1,0:T(8,128)(2,1)S(1)}, bf16[4,64,512]{2,1,0:T(8,128)(2,1)S(1)}, u32[]{:S(2)}, u32[]{:S(2)}) collective-permute-start(bf16[4,64,512]{2,1,0:T(8,128)(2,1)S(1)} %collective-permute-done.8.a_7_), channel_id=1, source_target_pairs={{0,1},{1,0},{2,3},{3,2},{4,5},{5,4},{6,7},{7,6},{8,9},{9,8},{10,11... | collective-permute-start | bytes 786440 | tf_op jit(solution)/shard_map/ppermute | solution.py:346
  41.9 6.7 %copy-start.13 = (bf16[4,64,512]{2,1,0:T(8,128)(2,1)}, bf16[4,64,512]{2,1,0:T(8,128)(2,1)S(1)}, u32[]{:S(2)}) copy-start(bf16[4,64,512]{2,1,0:T(8,128)(2,1)S(1)} %collective-permute-done.10.a_9_) | copy-start | bytes 786436
  41.9 6.6 %collective-permute-start.19 = (bf16[4,64,512]{2,1,0:T(8,128)(2,1)S(1)}, bf16[4,64,512]{2,1,0:T(8,128)(2,1)}, u32[]{:S(2)}, u32[]{:S(2)}) collective-permute-start(bf16[4,64,512]{2,1,0:T(8,128)(2,1)S(1)} %collective-permute-done.18.a_17_), channel_id=1, source_target_pairs={{0,1},{1,0},{2,3},{3,2},{4,5},{5,4},{6,7},{7,6},{8,9},{9,8},{10,11... | collective-permute-start | bytes 786440 | tf_op jit(solution)/shard_map/ppermute | solution.py:346
  42.3 1.1 copy-start.7
  42.3 6.2 %collective-permute-start.15 = (bf16[4,64,512]{2,1,0:T(8,128)(2,1)S(1)}, bf16[4,64,512]{2,1,0:T(8,128)(2,1)}, u32[]{:S(2)}, u32[]{:S(2)}) collective-permute-start(bf16[4,64,512]{2,1,0:T(8,128)(2,1)S(1)} %collective-permute-done.14.a_13_), channel_id=1, source_target_pairs={{0,1},{1,0},{2,3},{3,2},{4,5},{5,4},{6,7},{7,6},{8,9},{9,8},{10,11... | collective-permute-start | bytes 786440 | tf_op jit(solution)/shard_map/ppermute | solution.py:346
  42.4 6.2 %copy-start.14 = (bf16[4,64,512]{2,1,0:T(8,128)(2,1)}, bf16[4,64,512]{2,1,0:T(8,128)(2,1)S(1)}, u32[]{:S(2)}) copy-start(bf16[4,64,512]{2,1,0:T(8,128)(2,1)S(1)} %collective-permute-done.17.a_16_) | copy-start | bytes 786436
  42.4 6.1 %collective-permute-start.11 = (bf16[4,64,512]{2,1,0:T(8,128)(2,1)S(1)}, bf16[4,64,512]{2,1,0:T(8,128)(2,1)}, u32[]{:S(2)}, u32[]{:S(2)}) collective-permute-start(bf16[4,64,512]{2,1,0:T(8,128)(2,1)S(1)} %collective-permute-done.10.a_9_), channel_id=1, source_target_pairs={{0,1},{1,0},{2,3},{3,2},{4,5},{5,4},{6,7},{7,6},{8,9},{9,8},{10,11... | collective-permute-start | bytes 786440 | tf_op jit(solution)/shard_map/ppermute | solution.py:346
  48.4 0.7 copy-start.15
  48.5 0.8 copy-start.16
  63.3 15.6 %collective-permute-start.38 = (bf16[2,128,1024]{2,1,0:T(8,128)(2,1)}, bf16[2,128,1024]{2,1,0:T(8,128)(2,1)S(1)}, u32[]{:S(2)}, u32[]{:S(2)}) collective-permute-start(bf16[2,128,1024]{2,1,0:T(8,128)(2,1)} %get-tuple-element.67), channel_id=1, source_target_pairs={{0,8},{24,16},{1,9},{25,17},{2,10},{26,18},{3,11},{27,19},{4,12},{... | collective-permute-start | bytes 1572872 | tf_op jit(solution)/shard_map/ppermute | solution.py:381
  66.3 23.8 %collective-permute-start.31 = (bf16[2,128,1024]{2,1,0:T(8,128)(2,1)}, bf16[2,128,1024]{2,1,0:T(8,128)(2,1)S(1)}, u32[]{:S(2)}, u32[]{:S(2)}) collective-permute-start(bf16[2,128,1024]{2,1,0:T(8,128)(2,1)} %get-tuple-element.59), channel_id=1, source_target_pairs={{0,8},{24,16},{1,9},{25,17},{2,10},{26,18},{3,11},{27,19},{4,12},{... | collective-permute-start | bytes 1572872 | tf_op jit(solution)/shard_map/ppermute | solution.py:381
  67.6 33.7 %collective-permute-start.24 = (bf16[2,128,1024]{2,1,0:T(8,128)(2,1)}, bf16[2,128,1024]{2,1,0:T(8,128)(2,1)S(1)}, u32[]{:S(2)}, u32[]{:S(2)}) collective-permute-start(bf16[2,128,1024]{2,1,0:T(8,128)(2,1)} %get-tuple-element.51), channel_id=1, source_target_pairs={{0,8},{24,16},{1,9},{25,17},{2,10},{26,18},{3,11},{27,19},{4,12},{... | collective-permute-start | bytes 1572872 | tf_op jit(solution)/shard_map/ppermute | solution.py:381
  69.0 42.8 %collective-permute-start.20 = (bf16[2,128,1024]{2,1,0:T(8,128)(2,1)}, bf16[2,128,1024]{2,1,0:T(8,128)(2,1)S(1)}, u32[]{:S(2)}, u32[]{:S(2)}) collective-permute-start(bf16[2,128,1024]{2,1,0:T(8,128)(2,1)} %get-tuple-element.46), channel_id=1, source_target_pairs={{0,8},{24,16},{1,9},{25,17},{2,10},{26,18},{3,11},{27,19},{4,12},{... | collective-permute-start | bytes 1572872 | tf_op jit(solution)/shard_map/ppermute | solution.py:381
  80.1 40.3 %collective-permute-start.39 = (bf16[2,128,1024]{2,1,0:T(8,128)(2,1)S(1)}, bf16[2,128,1024]{2,1,0:T(8,128)(2,1)S(1)}, u32[]{:S(2)}, u32[]{:S(2)}) collective-permute-start(bf16[2,128,1024]{2,1,0:T(8,128)(2,1)S(1)} %add.81), channel_id=1, source_target_pairs={{8,16},{16,8},{9,17},{17,9},{10,18},{18,10},{11,19},{19,11},{12,20... | collective-permute-start | bytes 1572872 | tf_op jit(solution)/shard_map/ppermute | solution.py:381
  91.4 31.6 %collective-permute-start.32 = (bf16[2,128,1024]{2,1,0:T(8,128)(2,1)S(1)}, bf16[2,128,1024]{2,1,0:T(8,128)(2,1)S(1)}, u32[]{:S(2)}, u32[]{:S(2)}) collective-permute-start(bf16[2,128,1024]{2,1,0:T(8,128)(2,1)S(1)} %add.75), channel_id=1, source_target_pairs={{8,16},{16,8},{9,17},{17,9},{10,18},{18,10},{11,19},{19,11},{12,20... | collective-permute-start | bytes 1572872 | tf_op jit(solution)/shard_map/ppermute | solution.py:381
  102.6 23.1 %collective-permute-start.25 = (bf16[2,128,1024]{2,1,0:T(8,128)(2,1)S(1)}, bf16[2,128,1024]{2,1,0:T(8,128)(2,1)}, u32[]{:S(2)}, u32[]{:S(2)}) collective-permute-start(bf16[2,128,1024]{2,1,0:T(8,128)(2,1)S(1)} %add.69), channel_id=1, source_target_pairs={{8,16},{16,8},{9,17},{17,9},{10,18},{18,10},{11,19},{19,11},{12,20... | collective-permute-start | bytes 1572872 | tf_op jit(solution)/shard_map/ppermute | solution.py:381
  113.0 15.4 %collective-permute-start.21 = (bf16[2,128,1024]{2,1,0:T(8,128)(2,1)S(1)}, bf16[2,128,1024]{2,1,0:T(8,128)(2,1)S(1)}, u32[]{:S(2)}, u32[]{:S(2)}) collective-permute-start(bf16[2,128,1024]{2,1,0:T(8,128)(2,1)S(1)} %add.66), channel_id=1, source_target_pairs={{8,16},{16,8},{9,17},{17,9},{10,18},{18,10},{11,19},{19,11},{12,20... | collective-permute-start | bytes 1572872 | tf_op jit(solution)/shard_map/ppermute | solution.py:381
  121.6 19.5 %collective-permute-start.40 = (bf16[2,128,1024]{2,1,0:T(8,128)(2,1)S(1)}, bf16[2,128,1024]{2,1,0:T(8,128)(2,1)}, u32[]{:S(2)}, u32[]{:S(2)}) collective-permute-start(bf16[2,128,1024]{2,1,0:T(8,128)(2,1)S(1)} %add.82), channel_id=1, source_target_pairs={{16,24},{8,0},{17,25},{9,1},{18,26},{10,2},{19,27},{11,3},{20,28},... | collective-permute-start | bytes 1572872 | tf_op jit(solution)/shard_map/ppermute | solution.py:381
  124.2 31.9 %collective-permute-start.33 = (bf16[2,128,1024]{2,1,0:T(8,128)(2,1)S(1)}, bf16[2,128,1024]{2,1,0:T(8,128)(2,1)S(1)}, u32[]{:S(2)}, u32[]{:S(2)}) collective-permute-start(bf16[2,128,1024]{2,1,0:T(8,128)(2,1)S(1)} %add.76), channel_id=1, source_target_pairs={{16,24},{8,0},{17,25},{9,1},{18,26},{10,2},{19,27},{11,3},{20,28},... | collective-permute-start | bytes 1572872 | tf_op jit(solution)/shard_map/ppermute | solution.py:381
  127.1 36.4 %collective-permute-start.26 = (bf16[2,128,1024]{2,1,0:T(8,128)(2,1)S(1)}, bf16[2,128,1024]{2,1,0:T(8,128)(2,1)S(1)}, u32[]{:S(2)}, u32[]{:S(2)}) collective-permute-start(bf16[2,128,1024]{2,1,0:T(8,128)(2,1)S(1)} %add.70), channel_id=1, source_target_pairs={{16,24},{8,0},{17,25},{9,1},{18,26},{10,2},{19,27},{11,3},{20,28},... | collective-permute-start | bytes 1572872 | tf_op jit(solution)/shard_map/ppermute | solution.py:381
  129.6 43.5 %collective-permute-start.22 = (bf16[2,128,1024]{2,1,0:T(8,128)(2,1)S(1)}, bf16[2,128,1024]{2,1,0:T(8,128)(2,1)S(1)}, u32[]{:S(2)}, u32[]{:S(2)}) collective-permute-start(bf16[2,128,1024]{2,1,0:T(8,128)(2,1)S(1)} %add.67), channel_id=1, source_target_pairs={{16,24},{8,0},{17,25},{9,1},{18,26},{10,2},{19,27},{11,3},{20,28},... | collective-permute-start | bytes 1572872 | tf_op jit(solution)/shard_map/ppermute | solution.py:381
  143.6 32.8 %collective-permute-start.41 = (bf16[4,2,128,128]{3,2,1,0:T(8,128)(2,1)}, bf16[4,2,128,128]{3,2,1,0:T(8,128)(2,1)}, u32[]{:S(2)}, u32[]{:S(2)}) collective-permute-start(bf16[4,2,128,128]{3,2,1,0:T(8,128)(2,1)} %get-tuple-element.70), channel_id=1, source_target_pairs={{0,1},{1,0},{2,3},{3,2},{4,5},{5,4},{6,7},{7,6},{8,9},{9,8},{10,11... | collective-permute-start | bytes 786440 | tf_op jit(solution)/shard_map/ppermute | solution.py:346
  152.4 24.1 %copy-start.6 = (bf16[4,2,128,128]{3,2,1,0:T(8,128)(2,1)S(1)}, bf16[4,2,128,128]{3,2,1,0:T(8,128)(2,1)}, u32[]{:S(2)}) copy-start(bf16[4,2,128,128]{3,2,1,0:T(8,128)(2,1)} %get-tuple-element.69) | copy-start | bytes 786436
  156.1 0.8 copy-start.4
  159.4 41.5 %copy-start.17 = (f32[128,128,1]{0,1,2:T(8,128)S(1)}, f32[128,128,1]{0,1,2:T(8,128)}, u32[]{:S(2)}) copy-start(f32[128,128,1]{0,1,2:T(8,128)} %constant.28) | copy-start | bytes 196612
  159.4 20.4 %collective-permute-start.34 = (bf16[4,2,128,128]{3,2,1,0:T(8,128)(2,1)}, bf16[4,2,128,128]{3,2,1,0:T(8,128)(2,1)S(1)}, u32[]{:S(2)}, u32[]{:S(2)}) collective-permute-start(bf16[4,2,128,128]{3,2,1,0:T(8,128)(2,1)} %get-tuple-element.62), channel_id=1, source_target_pairs={{0,1},{1,0},{2,3},{3,2},{4,5},{5,4},{6,7},{7,6},{8,9},{9,8},{10,11... | collective-permute-start | bytes 786440 | tf_op jit(solution)/shard_map/ppermute | solution.py:346
  163.5 0.8 copy-start.3
  166.8 15.4 %collective-permute-start.27 = (bf16[4,2,128,128]{3,2,1,0:T(8,128)(2,1)}, bf16[4,2,128,128]{3,2,1,0:T(8,128)(2,1)S(1)}, u32[]{:S(2)}, u32[]{:S(2)}) collective-permute-start(bf16[4,2,128,128]{3,2,1,0:T(8,128)(2,1)} %get-tuple-element.54), channel_id=1, source_target_pairs={{0,1},{1,0},{2,3},{3,2},{4,5},{5,4},{6,7},{7,6},{8,9},{9,8},{10,11... | collective-permute-start | bytes 786440 | tf_op jit(solution)/shard_map/ppermute | solution.py:346
  173.1 0.8 copy-start.2
  176.4 8.3 %collective-permute-start.23 = (bf16[4,2,128,128]{3,2,1,0:T(8,128)(2,1)}, bf16[4,2,128,128]{3,2,1,0:T(8,128)(2,1)S(1)}, u32[]{:S(2)}, u32[]{:S(2)}) collective-permute-start(bf16[4,2,128,128]{3,2,1,0:T(8,128)(2,1)} %get-tuple-element.50), channel_id=1, source_target_pairs={{0,1},{1,0},{2,3},{3,2},{4,5},{5,4},{6,7},{7,6},{8,9},{9,8},{10,11... | collective-permute-start | bytes 786440 | tf_op jit(solution)/shard_map/ppermute | solution.py:346
  177.5 9.3 %collective-permute-start.42 = (bf16[2,128,128]{2,1,0:T(8,128)(2,1)S(1)}, bf16[2,128,128]{2,1,0:T(8,128)(2,1)S(1)}, u32[]{:S(2)}, u32[]{:S(2)}) collective-permute-start(bf16[2,128,128]{2,1,0:T(8,128)(2,1)S(1)} %get-tuple-element.72), channel_id=1, source_target_pairs={{0,2},{1,3},{2,0},{3,1},{4,6},{5,7},{6,4},{7,5},{8,10},{9,11},{10,... | collective-permute-start | bytes 196616 | tf_op jit(solution)/shard_map/ppermute | solution.py:346
  179.1 9.0 %collective-permute-start.43 = (bf16[2,128,128]{2,1,0:T(8,128)(2,1)S(1)}, bf16[2,128,128]{2,1,0:T(8,128)(2,1)S(1)}, u32[]{:S(2)}, u32[]{:S(2)}) collective-permute-start(bf16[2,128,128]{2,1,0:T(8,128)(2,1)S(1)} %get-tuple-element.73), channel_id=1, source_target_pairs={{0,4},{1,5},{2,6},{3,7},{4,0},{5,1},{6,2},{7,3},{8,12},{9,13},{10,... | collective-permute-start | bytes 196616 | tf_op jit(solution)/shard_map/ppermute | solution.py:346
  179.9 9.7 %collective-permute-start.44 = (bf16[2,128,128]{2,1,0:T(8,128)(2,1)S(1)}, bf16[2,128,128]{2,1,0:T(8,128)(2,1)S(1)}, u32[]{:S(2)}, u32[]{:S(2)}) collective-permute-start(bf16[2,128,128]{2,1,0:T(8,128)(2,1)S(1)} %get-tuple-element.74), channel_id=1, source_target_pairs={{0,6},{1,7},{2,4},{3,5},{4,2},{5,3},{6,0},{7,1},{8,14},{9,15},{10,... | collective-permute-start | bytes 196616 | tf_op jit(solution)/shard_map/ppermute | solution.py:346
  182.2 8.3 %collective-permute-start.35 = (bf16[2,128,128]{2,1,0:T(8,128)(2,1)S(1)}, bf16[2,128,128]{2,1,0:T(8,128)(2,1)S(1)}, u32[]{:S(2)}, u32[]{:S(2)}) collective-permute-start(bf16[2,128,128]{2,1,0:T(8,128)(2,1)S(1)} %get-tuple-element.64), channel_id=1, source_target_pairs={{0,2},{1,3},{2,0},{3,1},{4,6},{5,7},{6,4},{7,5},{8,10},{9,11},{10,... | collective-permute-start | bytes 196616 | tf_op jit(solution)/shard_map/ppermute | solution.py:346
  184.8 7.0 %collective-permute-start.36 = (bf16[2,128,128]{2,1,0:T(8,128)(2,1)S(1)}, bf16[2,128,128]{2,1,0:T(8,128)(2,1)S(1)}, u32[]{:S(2)}, u32[]{:S(2)}) collective-permute-start(bf16[2,128,128]{2,1,0:T(8,128)(2,1)S(1)} %get-tuple-element.65), channel_id=1, source_target_pairs={{0,4},{1,5},{2,6},{3,7},{4,0},{5,1},{6,2},{7,3},{8,12},{9,13},{10,... | collective-permute-start | bytes 196616 | tf_op jit(solution)/shard_map/ppermute | solution.py:346
  186.8 6.0 %collective-permute-start.37 = (bf16[2,128,128]{2,1,0:T(8,128)(2,1)S(1)}, bf16[2,128,128]{2,1,0:T(8,128)(2,1)S(1)}, u32[]{:S(2)}, u32[]{:S(2)}) collective-permute-start(bf16[2,128,128]{2,1,0:T(8,128)(2,1)S(1)} %get-tuple-element.66), channel_id=1, source_target_pairs={{0,6},{1,7},{2,4},{3,5},{4,2},{5,3},{6,0},{7,1},{8,14},{9,15},{10,... | collective-permute-start | bytes 196616 | tf_op jit(solution)/shard_map/ppermute | solution.py:346
  188.1 6.8 %collective-permute-start.28 = (bf16[4,128,128]{2,1,0:T(8,128)(2,1)S(1)}, bf16[4,128,128]{2,1,0:T(8,128)(2,1)S(1)}, u32[]{:S(2)}, u32[]{:S(2)}) collective-permute-start(bf16[4,128,128]{2,1,0:T(8,128)(2,1)S(1)} %get-tuple-element.56), channel_id=1, source_target_pairs={{0,2},{1,3},{2,0},{3,1},{4,6},{5,7},{6,4},{7,5},{8,10},{9,11},{10,... | collective-permute-start | bytes 393224 | tf_op jit(solution)/shard_map/ppermute | solution.py:346
  189.6 7.5 %collective-permute-start.29 = (bf16[4,128,128]{2,1,0:T(8,128)(2,1)S(1)}, bf16[4,128,128]{2,1,0:T(8,128)(2,1)S(1)}, u32[]{:S(2)}, u32[]{:S(2)}) collective-permute-start(bf16[4,128,128]{2,1,0:T(8,128)(2,1)S(1)} %get-tuple-element.57), channel_id=1, source_target_pairs={{0,4},{1,5},{2,6},{3,7},{4,0},{5,1},{6,2},{7,3},{8,12},{9,13},{10,... | collective-permute-start | bytes 393224 | tf_op jit(solution)/shard_map/ppermute | solution.py:346
  190.5 6.6 %collective-permute-start.30 = (bf16[4,128,128]{2,1,0:T(8,128)(2,1)S(1)}, bf16[4,128,128]{2,1,0:T(8,128)(2,1)S(1)}, u32[]{:S(2)}, u32[]{:S(2)}) collective-permute-start(bf16[4,128,128]{2,1,0:T(8,128)(2,1)S(1)} %pad_maximum_fusion.5), channel_id=1, source_target_pairs={{0,6},{1,7},{2,4},{3,5},{4,2},{5,3},{6,0},{7,1},{8,14},{9,15},{10,... | collective-permute-start | bytes 393224 | tf_op jit(solution)/shard_map/ppermute | solution.py:346
  197.2 3.8 %collective-permute-start.45 = (bf16[4,128,128]{2,1,0:T(8,128)(2,1)S(1)}, bf16[4,128,128]{2,1,0:T(8,128)(2,1)S(1)}, u32[]{:S(2)}, u32[]{:S(2)}) collective-permute-start(bf16[4,128,128]{2,1,0:T(8,128)(2,1)S(1)} %pad_maximum_fusion.6), channel_id=1, source_target_pairs={{0,8},{24,16},{1,9},{25,17},{2,10},{26,18},{3,11},{27,19},{4,12},{... | collective-permute-start | bytes 393224 | tf_op jit(solution)/shard_map/ppermute | solution.py:430
